TPU v7x, 8 devices: a whole 2x2x1 slice. The times are simulated.
8 devices in a mesh: dp: 1 (over z), pool: 2 (over y), ep: 4 (over x, core).
Axes of the slice: x: 2, y: 2, z: 1, core: 2. Of those that a mesh axis runs over, the one named last changes fastest.
Arguments:
- hidden_in: bfloat16 [512, 896], P(('dp', 'ep'))
- k_cache: bfloat16 [2, 512, 512, 2, 128], P(None, ('dp', 'ep'), 'pool')
- v_cache: bfloat16 [2, 512, 512, 2, 128], P(None, ('dp', 'ep'), 'pool')
- cache_len: int32 [512], P(('dp', 'ep'))
- w_q: bfloat16 [2, 896, 2048], replicated
- w_k: bfloat16 [2, 896, 256], replicated
- w_v: bfloat16 [2, 896, 256], replicated
- w_o: bfloat16 [2, 2048, 896], replicated
- w_router: float32 [2, 896, 256], replicated
- expert_ids: int32 [2, 512, 8], P(None, ('dp', 'ep'))
- w_one: bfloat16 [2, 256, 896, 256], P(None, 'ep', None, 'pool')
- w_three: bfloat16 [2, 256, 896, 256], P(None, 'ep', None, 'pool')
- w_two: bfloat16 [2, 256, 256, 896], P(None, 'ep', 'pool')
Outputs:
- output: bfloat16 [512, 896], P(('dp', 'ep'))
All inputs are finite; a program needn't handle non-finite values.
Results may differ from a plain program's by a relative error of at most 0.02.
Values are sent between devices in bfloat16 or wider.
A program may use at most 1 GiB of HBM per device.

v0:
```python
import functools

import jax
import jax.numpy as jnp
from jax import lax
from jax.experimental import pallas as pl
from jax.experimental.pallas import tpu as pltpu
from jax.sharding import PartitionSpec as P

MESH = pl.DeviceIdType.MESH
F32, BF16, I32 = jnp.float32, jnp.bfloat16, jnp.int32
NORM_EPS = 1e-6
T, D, HD, H = 128, 896, 128, 16
HALF = T // 2
KV = 2
POS = 256
ROWS = POS * KV
CH = 8
NCH = T // CH
NB = 8
ALL = 4 * T
NE = 64
PAIRS = 1024
FF = 128
NW = 32
MC = 32
CM = 384
PARTS = 2
NR = PAIRS // PARTS
PR = 3 * NR + NR // 2
PAD = MC
MIB = 1024 * 1024


def rms(v):
    v = v.astype(F32)
    return v * lax.rsqrt(jnp.mean(v * v, axis=-1, keepdims=True) + NORM_EPS)


def mm(a, b):
    return jnp.dot(a, b, preferred_element_type=F32)


def iota(shape, dim):
    return lax.broadcasted_iota(I32, shape, dim)


def peers():
    g, p, e = lax.axis_index("dp"), lax.axis_index("pool"), lax.axis_index("ep")
    core = lax.rem(e, 2)
    e_x = lax.rem(e + 2, 4)
    e_d = e + 1 - 2 * core
    e_z = lax.rem(e_d + 2, 4)
    return p, e, e_x, e_d, e_z, (g, 1 - p, e), (g, p, e_x), (g, p, e_d), (g, p, e_z), (g, 1 - p, e_x)


def entry_barrier(targets):
    bar = pltpu.get_barrier_semaphore()
    for dev in targets:
        pl.semaphore_signal(bar, inc=1, device_id=dev, device_id_type=MESH)
    pl.semaphore_wait(bar, len(targets))


def remote(src, dst, send_sem, recv_sem, dev):
    return pltpu.make_async_remote_copy(src_ref=src, dst_ref=dst, send_sem=send_sem, recv_sem=recv_sem,
                                        device_id=dev, device_id_type=MESH)


def route(ids, e, meta, pos):
    sub = iota((128, ALL), 0)
    local = [ids[k:k + 1, :] - e * NE for k in range(8)]
    local = [jnp.where((v >= 0) & (v < NE), v, -1) for v in local]
    mask = jnp.zeros((128, ALL), F32)
    for v in local:
        mask = jnp.where(v == sub, 1.0, mask)
    mask_b = mask.astype(BF16)
    before = (iota((ALL, ALL), 0) < iota((ALL, ALL), 1)).astype(BF16)
    rank = mm(mask_b, before)
    n_col = jnp.broadcast_to(jnp.sum(mask, axis=1, keepdims=True), (128, 128)).astype(I32)
    n_row = lax.dot_general(jnp.ones((8, ALL), BF16), mask_b, (((1,), (1,)), ((), ())),
                            preferred_element_type=F32).astype(I32)
    lower = (iota((128, 128), 1) < iota((128, 128), 0)).astype(BF16)
    upper = (iota((128, 128), 0) < iota((128, 128), 1)).astype(BF16)
    as_b = lambda v: v.astype(F32).astype(BF16)
    off_col = mm(lower, as_b((n_col + 15) >> 4)) * 16.0
    offc_col = mm(lower, as_b(n_col >> 4)) * 16.0 + mm(lower, as_b(n_col & 15))
    off_row = mm(as_b((n_row + 15) >> 4), upper).astype(I32)
    offc_row = (mm(as_b(n_row >> 4), upper) * 16.0 + mm(as_b(n_row & 15), upper)).astype(I32)
    real = iota((8, 128), 1) < NE
    table = [n_row, off_row, offc_row]
    for r in range(PARTS):
        lo = jnp.sum(jnp.where(real & (offc_row + n_row <= r * NR), 1.0, 0.0), axis=1, keepdims=True)
        hi = jnp.sum(jnp.where(real & (offc_row < (r + 1) * NR), 1.0, 0.0), axis=1, keepdims=True)
        table.append(jnp.where(iota((8, 128), 1) == 0, lo, hi).astype(I32))
    row = iota((8, 128), 0)
    packed = jnp.zeros((8, 128), I32)
    for i, v in enumerate(table):
        packed = jnp.where(row == i, v, packed)
    meta[...] = packed
    for base, off in ((0, off_col), (8, offc_col)):
        where_to = off[:, 0:1] + rank + 1.0
        for k in range(8):
            found = jnp.sum(jnp.where(local[k] == sub, where_to, 0.0), axis=0, keepdims=True)
            pos[base + k:base + k + 1, :] = (found - 1.0).astype(I32)


def attn_kernel(layer, first, *refs):
    if first:
        (x_ref, len_ref, idt_ref, k_ref, v_ref, wq_ref, wk_ref, wv_ref, wo_ref, a_ref, ida_ref, meta_ref, pos_ref, *scr) = refs
    else:
        (x_ref, len_ref, k_ref, v_ref, wq_ref, wk_ref, wv_ref, wo_ref, a_ref, *scr) = refs
    (kbuf, vbuf, wq_v, wk_v, wv_v, wo_v, q2d, kn2d, vn2d, num, nrec, stat, ssend, srec,
     kv_sem, w_sem, ns_sem, nr_sem, ss_sem, sr_sem, gs_sem, gr_sem, is_sem, ir_sem) = scr
    p, e, e_x, e_d, e_z, dev_y, dev_x, dev_d, dev_z, dev_yx = peers()

    def tok_of(c):
        first_half = (1 - p) * HALF + c * CH
        second_half = p * HALF + (c - NCH // 2) * CH
        return pl.multiple_of(jnp.where(c < NCH // 2, first_half, second_half), CH)

    def kv_copies(c):
        slot = c & (NB - 1)
        src = pl.ds(tok_of(c), CH)
        return (pltpu.make_async_copy(k_ref.at[layer, src], kbuf.at[slot], kv_sem.at[0, slot]),
                pltpu.make_async_copy(v_ref.at[layer, src], vbuf.at[slot], kv_sem.at[1, slot]))

    weights = [pltpu.make_async_copy(r.at[layer], b, w_sem.at[i])
               for i, (r, b) in enumerate(((wq_ref, wq_v), (wk_ref, wk_v), (wv_ref, wv_v), (wo_ref, wo_v)))]
    for cp in weights[:3]:
        cp.start()
    for c in range(2):
        for cp in kv_copies(jnp.int32(c)):
            cp.start()

    entry_barrier((dev_y, dev_x, dev_d, dev_z, dev_yx))

    id_copies = []
    if first:
        mine = (slice(None), slice(None), pl.ds(pl.multiple_of(e * T, T), T))
        ida_ref[mine] = idt_ref[...]
        for i, dev in enumerate((dev_x, dev_d, dev_z)):
            id_copies.append(remote(idt_ref, ida_ref.at[mine], is_sem.at[i], ir_sem.at[i], dev))
            id_copies[-1].start()

    normed = rms(x_ref[...]).astype(BF16)
    for cp in weights[:3]:
        cp.wait()
    for c in range(2, NB):
        for cp in kv_copies(jnp.int32(c)):
            cp.start()
    weights[3].start()
    for hp in range(H // 2):
        pair = mm(normed, wq_v[:, hp * 256:(hp + 1) * 256]).astype(BF16).astype(F32)
        for i in range(2):
            q2d[pl.ds(hp * 2 + i, T, stride=H), :] = pair[:, i * HD:(i + 1) * HD]
    for w, dst in ((wk_v, kn2d), (wv_v, vn2d)):
        pair = mm(normed, w[...]).astype(BF16).astype(F32)
        for i in range(KV):
            dst[pl.ds(i, T, stride=KV), :] = pair[:, i * HD:(i + 1) * HD]

    scale = HD ** -0.5
    col = iota((H, ROWS), 1)
    group_ok = (col & 1) == (iota((H, ROWS), 0) // (H // KV))
    col_pos = jnp.where(group_ok, col >> 1, 1 << 30)
    lane = iota((H, T), 1)

    def heads_of(ref, tok):
        two = ref[pl.ds(tok * KV, KV), :]
        return jnp.concatenate([jnp.broadcast_to(two[i:i + 1], (H // KV, HD)) for i in range(KV)], axis=0)

    def num_copy(c):
        rows = pl.ds(pl.multiple_of(c * (CH * H), CH * H), CH * H)
        return remote(num.at[rows], nrec.at[rows], ns_sem.at[c], nr_sem.at[c], dev_y)

    stat_copy = remote(ssend, srec, ss_sem, sr_sem, dev_y)

    def chunk(c, carry):
        slot = c & (NB - 1)
        for cp in kv_copies(c):
            cp.wait()
        tok0 = tok_of(c)
        m_all, l_all, n_all = stat[0], stat[1], stat[2]
        for j0 in range(0, CH, 4):
            group = range(j0, j0 + 4)
            qs, ss = {}, {}
            for j in group:
                qs[j] = q2d[pl.ds(pl.multiple_of((tok0 + j) * H, H), H), :]
                ss[j] = lax.dot_general(qs[j].astype(BF16), kbuf[slot, j], (((1,), (1,)), ((), ())),
                                        preferred_element_type=F32) * scale
            ps = {}
            for j in group:
                limit = len_ref[tok0 + j] - p * POS
                s = jnp.where(col_pos < limit, ss[j], -1e30)
                s_new = jnp.sum(qs[j] * heads_of(kn2d, tok0 + j), axis=1, keepdims=True) * scale
                m = jnp.maximum(jnp.max(s, axis=1, keepdims=True), s_new)
                pr = jnp.exp(s - m)
                ps[j] = pr.astype(BF16)
                here = lane == c * CH + j
                m_all = jnp.where(here, m, m_all)
                l_all = jnp.where(here, jnp.sum(pr, axis=1, keepdims=True), l_all)
                n_all = jnp.where(here, s_new, n_all)
            for j in group:
                num[pl.ds(pl.multiple_of((c * CH + j) * H, H), H), :] = mm(ps[j], vbuf[slot, j])
        stat[0], stat[1], stat[2] = m_all, l_all, n_all

        @pl.when(c + NB < NCH)
        def _():
            for cp in kv_copies(c + NB):
                cp.start()

        @pl.when(c == NCH // 2 - 1)
        def _():
            ssend[0], ssend[1] = m_all, l_all

        @pl.when((c >= 1) & (c <= NCH // 2))
        def _():
            num_copy(c - 1).start()

        @pl.when(c == NCH // 2)
        def _():
            stat_copy.start()

        return carry

    stat[...] = jnp.zeros_like(stat)
    lax.fori_loop(0, NCH, chunk, 0)

    weights[3].wait()
    stat_copy.wait()
    m_own, l_own, s_new = stat[0], stat[1], stat[2]
    m_far = pltpu.roll(srec[0], HALF, axis=1)
    l_far = pltpu.roll(srec[1], HALF, axis=1)
    m = jnp.maximum(m_own, m_far)
    w_own, w_far, w_new = jnp.exp(m_own - m), jnp.exp(m_far - m), jnp.exp(s_new - m)
    denom = l_own * w_own + l_far * w_far + w_new
    c_own, c_far, c_new = w_own / denom, w_far / denom, w_new / denom

    def combine(c, carry):
        num_copy(c).wait()
        for j in range(CH):
            i = c * CH + j
            pick = lane == HALF + i
            own, far, new = [jnp.sum(jnp.where(pick, v, 0.0), axis=1, keepdims=True) for v in (c_own, c_far, c_new)]
            there = pl.ds(pl.multiple_of(i * H, H), H)
            here = pl.ds(pl.multiple_of((HALF + i) * H, H), H)
            num[here, :] = num[here, :] * own + nrec[there, :] * far + heads_of(vn2d, p * HALF + i) * new
        return carry

    lax.fori_loop(0, NCH // 2, combine, 0)

    proj = jnp.zeros((HALF, D), F32)
    for hp in range(H // 2):
        pair = jnp.concatenate([num[pl.ds(HALF * H + hp * 2 + i, HALF, stride=H), :].astype(BF16) for i in range(2)], axis=1)
        proj = proj + mm(pair, wo_v[hp * 256:(hp + 1) * 256, :])
    mine = pl.ds(pl.multiple_of(p * HALF, HALF), HALF)

    def rows(pp, ee):
        return pl.ds(pl.multiple_of(ee * T + pp * HALF, HALF), HALF)

    a_ref[rows(p, e), :] = (x_ref[mine, :].astype(F32) + proj).astype(BF16)

    def gather(i, pp, ee, dev):
        block = a_ref.at[rows(pp, ee)]
        cp = remote(block, block, gs_sem.at[i], gr_sem.at[i], dev)
        cp.start()
        return cp

    copies = [gather(0, p, e, dev_yx), gather(1, p, e, dev_x), gather(2, p, e, dev_y), gather(3, p, e, dev_d)]
    if first:
        for cp in id_copies:
            cp.wait()
        for n in range(ida_ref.shape[0]):
            route(ida_ref.at[n], e, meta_ref.at[n], pos_ref.at[n])
    for i, pp, ee in ((2, 1 - p, e), (1, p, e_x), (0, 1 - p, e_x)):
        copies[i].wait_recv()
        copies.append(gather(len(copies), pp, ee, dev_d))
    for i in range(3, 7):
        copies[i].wait_recv()
    for cp in copies:
        cp.wait_send()


def attention(layer, x, cache_len, id_t, k, v, wq, wk, wv, wo, cid):
    first = id_t is not None
    vm, sm, hb = (pl.BlockSpec(memory_space=m) for m in (pltpu.VMEM, pltpu.SMEM, pltpu.HBM))
    dma = pltpu.SemaphoreType.DMA
    outs = [jax.ShapeDtypeStruct((ALL, D), BF16)]
    if first:
        layers = id_t.shape[0]
        outs += [jax.ShapeDtypeStruct((layers, 8, ALL), I32), jax.ShapeDtypeStruct((layers, 8, 128), I32),
                 jax.ShapeDtypeStruct((layers, 16, ALL), I32)]
    out = pl.pallas_call(
        functools.partial(attn_kernel, layer, first),
        name=f"attn_{layer}",
        out_shape=outs,
        in_specs=[vm, sm] + ([vm] if first else []) + [hb] * 6,
        out_specs=[vm] * len(outs),
        scratch_shapes=[
            pltpu.VMEM((NB, CH, ROWS, HD), BF16), pltpu.VMEM((NB, CH, ROWS, HD), BF16),
            pltpu.VMEM((D, H * HD), BF16), pltpu.VMEM((D, KV * HD), BF16), pltpu.VMEM((D, KV * HD), BF16),
            pltpu.VMEM((H * HD, D), BF16),
            pltpu.VMEM((T * H, HD), F32), pltpu.VMEM((T * KV, HD), F32), pltpu.VMEM((T * KV, HD), F32),
            pltpu.VMEM((T * H, HD), F32), pltpu.VMEM((HALF * H, HD), F32),
            pltpu.VMEM((3, H, T), F32), pltpu.VMEM((2, H, T), F32), pltpu.VMEM((2, H, T), F32),
            dma((2, NB)), dma((4,)), dma((NCH // 2,)), dma((NCH // 2,)), dma(()), dma(()),
            dma((7,)), dma((7,)), dma((3,)), dma((3,)),
        ],
        compiler_params=pltpu.CompilerParams(collective_id=cid, has_side_effects=True, vmem_limit_bytes=61 * MIB),
    )(*([x, cache_len] + ([id_t] if first else []) + [k, v, wq, wk, wv, wo]))
    return out


def expert_kernel(layer, part, a_ref, meta, pos_ref, w1_ref, w3_ref, w2_ref, mine_ref, theirs_ref,
                  w1b, w3b, w2b, u, xs, ym, yt, tail, w_sem, o_sem):
    p = lax.axis_index("pool")
    r0 = part * NR
    lo, hi = meta[layer, 3 + part, 0], meta[layer, 3 + part, 1]
    odd = (hi - lo) & 1
    lo, hi = jnp.where((odd == 1) & (hi == NE), lo - 1, lo), jnp.where((odd == 1) & (hi < NE), hi + 1, hi)

    def w_copies(i):
        slot = i & (NW - 1)
        return [pltpu.make_async_copy(r.at[layer, i], b.at[slot], w_sem.at[n, slot])
                for n, (r, b) in enumerate(((w1_ref, w1b), (w3_ref, w3b), (w2_ref, w2b)))]

    def start(i, carry):
        for cp in w_copies(i):
            cp.start()
        return carry

    lax.fori_loop(lo, jnp.minimum(lo + NW, hi), start, 0)

    u[...] = rms(a_ref[...]).astype(BF16)

    def dispatch(i, carry):
        row = iota((256, ALL), 0) + i * 256
        hit = jnp.zeros((256, ALL), F32)
        for k in range(8):
            hit = jnp.where(pos_ref[layer, k:k + 1, :] == row, 1.0, hit)
        xs[pl.ds(pl.multiple_of(i * 256, 256), 256), :] = mm(hit.astype(BF16), u[...]).astype(BF16)
        return carry

    lax.fori_loop(meta[layer, 1, lo] >> 4, (meta[layer, 1, hi] + 15) >> 4, dispatch, 0)

    def rows_at(i, j):
        slot = i & (NW - 1)
        rows = xs[pl.ds(pl.multiple_of(meta[layer, 1, i] * 16 + j * MC, 16), MC), :]
        act = (jax.nn.silu(mm(rows, w1b[slot])) * mm(rows, w3b[slot])).astype(BF16)
        return mm(act, w2b[slot]), pl.ds(jnp.minimum(meta[layer, 2, i] + j * MC - r0, NR) + PAD, MC)

    def targets(to):
        return [ym.at[t // 3, t % 3, to] for t in range(6)] + [yt.at[to]]

    def first_step(i):
        return jnp.maximum(r0 - meta[layer, 2, i], 0) >> 5

    def more_steps(i):
        n, offc, first = meta[layer, 0, i], meta[layer, 2, i], first_step(i)

        def step(j, carry):
            y, to = rows_at(i, j)
            keep = iota((MC, 128), 0) < n - j * MC
            for t, ref in enumerate(targets(to)):
                ref[...] = jnp.where(keep, y[:, t * 128:(t + 1) * 128], ref[...])
            return carry

        lax.fori_loop(first + 1, (jnp.minimum(n, r0 + NR - offc) + MC - 1) >> 5, step, 0)

    def expert_pair(h, carry):
        pair = [lo + 2 * h, lo + 2 * h + 1]
        for i in pair:
            for cp in w_copies(i):
                cp.wait()
        done = [rows_at(i, first_step(i)) for i in pair]
        for y, to in done:
            for t, ref in enumerate(targets(to)):
                ref[...] = y[:, t * 128:(t + 1) * 128]
        for i in pair:
            more_steps(i)
        for i in pair:
            @pl.when(i + NW < hi)
            def _():
                start(i + NW, 0)
        return carry

    lax.fori_loop(0, (hi - lo) >> 1, expert_pair, 0)
    copies = []
    for n, (q, ref) in enumerate(((1 - p, theirs_ref), (p, mine_ref))):
        for t in range(3):
            copies.append(pltpu.make_async_copy(ym.at[q, t, pl.ds(PAD, NR)], ref.at[pl.ds(t * NR, NR)], o_sem.at[n, t]))
            copies[-1].start()
    top, bot = yt[PAD:PAD + NR // 2, :], yt[PAD + NR // 2:PAD + NR, :]
    left = iota((NR // 2, 128), 1) < 64
    tail[0] = jnp.where(left, top, pltpu.roll(bot, 64, axis=1))
    tail[1] = jnp.where(left, pltpu.roll(top, 64, axis=1), bot)
    for n, (q, ref) in enumerate(((1 - p, theirs_ref), (p, mine_ref))):
        copies.append(pltpu.make_async_copy(tail.at[q], ref.at[pl.ds(3 * NR, NR // 2)], o_sem.at[n, 3]))
        copies[-1].start()
    for cp in copies:
        cp.wait()


def experts(layer, part, a_all, meta, pos, w1, w3, w2):
    vm, sm, hb, anywhere = (pl.BlockSpec(memory_space=m) for m in (pltpu.VMEM, pltpu.SMEM, pltpu.HBM, pl.ANY))
    dma = pltpu.SemaphoreType.DMA
    return pl.pallas_call(
        functools.partial(expert_kernel, layer, part),
        name=f"experts_{layer}_{part}",
        out_shape=[jax.ShapeDtypeStruct((PR, 128), F32)] * 2,
        in_specs=[vm, sm, vm, hb, hb, hb],
        out_specs=[anywhere, anywhere],
        scratch_shapes=[
            pltpu.VMEM((NW, D, FF), BF16), pltpu.VMEM((NW, D, FF), BF16), pltpu.VMEM((NW, FF, D), BF16),
            pltpu.VMEM((ALL, D), BF16), pltpu.VMEM((2304, D), BF16),
            pltpu.VMEM((2, 3, NR + 2 * PAD, 128), F32), pltpu.VMEM((NR + 2 * PAD, 128), F32),
            pltpu.VMEM((2, NR // 2, 128), F32),
            dma((3, NW)), dma((2, 4)),
        ],
        compiler_params=pltpu.CompilerParams(vmem_limit_bytes=38 * MIB),
        cost_estimate=pl.CostEstimate(flops=4_000_000_000, bytes_accessed=44_000_000 // PARTS, transcendentals=PAIRS * FF // PARTS),
    )(a_all, meta, pos, w1, w3, w2)


def merge_kernel(layer, a_ref, id_ref, pos_ref, mine0_ref, far0_ref, mine1_ref, theirs1_ref, wr_ref, x_ref,
                 y_own, y_far, wr, gate, base, acc, back, xsend, xfar,
                 l_sem, ys_sem, yr_sem, bs_sem, br_sem, fs_sem, fr_sem):
    p, e, e_x, e_d, e_z, dev_y, dev_x, dev_d, dev_z, dev_yx = peers()
    loads = [pltpu.make_async_copy(src, dst, l_sem.at[i])
             for i, (src, dst) in enumerate(((wr_ref.at[layer], wr), (mine0_ref, y_own.at[0]), (far0_ref, y_far.at[0]),
                                             (mine1_ref, y_own.at[1])))]
    for cp in loads:
        cp.start()
    entry_barrier((dev_y, dev_x, dev_d, dev_z))
    spans = [(t * NR, NR) for t in range(3)] + [(3 * NR, NR // 2)]
    y_copies = [remote(theirs1_ref.at[pl.ds(b, n)], y_far.at[1, pl.ds(b, n)], ys_sem.at[t], yr_sem.at[t], dev_y)
                for t, (b, n) in enumerate(spans)]
    for cp in y_copies:
        cp.start()

    loads[0].wait()
    u = rms(a_ref[...]).astype(BF16)
    logits = jnp.zeros((ALL, 256), F32)
    rest = wr[...]
    for _ in range(3):
        part = rest.astype(BF16)
        rest = rest - part.astype(F32)
        logits = logits + mm(u, part)
    col = iota((ALL, 256), 1)
    g = [jnp.sum(jnp.where(id_ref[layer, :, k:k + 1] == col, logits, 0.0), axis=1, keepdims=True) for k in range(8)]
    top = functools.reduce(jnp.maximum, g)
    g = [jnp.exp(v - top) for v in g]
    total = functools.reduce(jnp.add, g)
    g = [v / total for v in g]
    pos = [pos_ref[layer, :, 8 + k:9 + k] for k in range(8)]
    lane = iota((ALL, 128), 1)
    for c in range(PAIRS // 128):
        w = jnp.zeros((ALL, 128), F32)
        for k in range(8):
            w = jnp.where(pos[k] == lane + c * 128, g[k], w)
        for i in range(3):
            part = w.astype(BF16)
            w = w - part.astype(F32)
            gate[i, :, c * 128:(c + 1) * 128] = part

    def mix(h, t):
        b, n = spans[t]
        y = (y_own[h, b:b + n, :] + y_far[h, b:b + n, :]).astype(BF16)
        first = h * NR
        if t < 3:
            return sum(mm(gate[i, :, first:first + NR], y) for i in range(3))
        lo, hi = [sum(mm(gate[i, :, first + q * n:first + (q + 1) * n], y) for i in range(3)) for q in range(2)]
        keep = jnp.broadcast_to(p == 0, lo.shape)
        return jnp.where(keep, lo, pltpu.roll(lo, 64, axis=1)) + jnp.where(keep, pltpu.roll(hi, 64, axis=1), hi)

    loads[1].wait()
    loads[2].wait()
    for t in range(4):
        base[t] = mix(0, t)
    loads[3].wait()

    def block_of(ee):
        return pl.ds(pl.multiple_of(ee * T, T), T)

    def give(t):
        cps = [remote(acc.at[t, block_of(ee)], back.at[t, i], bs_sem.at[t, i], br_sem.at[t, i], dev)
               for i, (ee, dev) in enumerate(((e_x, dev_x), (e_z, dev_z), (e_d, dev_d)))]
        for cp in cps:
            cp.start()
        return cps

    def cols(q, t):
        return pl.ds(pl.multiple_of(q * CM + t * 128, 128), 128) if t < 3 else slice(2 * CM, D)

    def finish(t, cps):
        for cp in cps:
            cp.wait_recv()
        total = acc[t, block_of(e), :] + back[t, 0] + back[t, 1] + back[t, 2]
        xsend[t] = (a_ref[block_of(e), cols(p, t)].astype(F32) + total).astype(BF16)
        cp = remote(xsend.at[t], xfar.at[t], fs_sem.at[t], fr_sem.at[t], dev_y)
        cp.start()
        return cp

    given, sent = [], []
    for t in range(4):
        y_copies[t].wait_recv()
        acc[t] = base[t] + mix(1, t)
        given.append(give(t))
        if t >= 1:
            sent.append(finish(t - 1, given[t - 1]))
    sent.append(finish(3, given[3]))
    for t in range(3):
        x_ref[:, cols(p, t)] = xsend[t]
        sent[t].wait()
        x_ref[:, cols(1 - p, t)] = xfar[t]
    sent[3].wait()
    keep_own = (iota((T, 128), 1) // 64) == p
    x_ref[:, 2 * CM:] = jnp.where(keep_own, xsend[3].astype(F32), xfar[3].astype(F32)).astype(BF16)
    for cp in y_copies + [c for cps in given for c in cps]:
        cp.wait_send()


def merge(layer, a_all, ids, pos, mine0, far0, mine1, theirs1, wr, cid):
    vm, hb, anywhere = (pl.BlockSpec(memory_space=m) for m in (pltpu.VMEM, pltpu.HBM, pl.ANY))
    dma = pltpu.SemaphoreType.DMA
    return pl.pallas_call(
        functools.partial(merge_kernel, layer),
        name=f"merge_{layer}",
        out_shape=jax.ShapeDtypeStruct((T, D), BF16),
        in_specs=[vm, vm, vm, anywhere, anywhere, anywhere, anywhere, hb],
        out_specs=vm,
        scratch_shapes=[
            pltpu.VMEM((2, PR, 128), F32), pltpu.VMEM((2, PR, 128), F32),
            pltpu.VMEM((D, 256), F32), pltpu.VMEM((3, ALL, PAIRS), BF16),
            pltpu.VMEM((4, ALL, 128), F32), pltpu.VMEM((4, ALL, 128), F32), pltpu.VMEM((4, 3, T, 128), F32),
            pltpu.VMEM((4, T, 128), BF16), pltpu.VMEM((4, T, 128), BF16),
            dma((4,)), dma((4,)), dma((4,)), dma((4, 3)), dma((4, 3)), dma((4,)), dma((4,)),
        ],
        compiler_params=pltpu.CompilerParams(collective_id=cid, has_side_effects=True, vmem_limit_bytes=24 * MIB),
    )(a_all, ids, pos, mine0, far0, mine1, theirs1, wr)


def solution(mesh):
    tok_spec = P(('dp', 'ep'), None)
    cache_spec = P(None, ('dp', 'ep'), 'pool', None, None)
    up_spec = P(None, 'ep', None, 'pool')
    down_spec = P(None, 'ep', 'pool', None)
    in_specs = (tok_spec, cache_spec, cache_spec, P(('dp', 'ep')), P(), P(), P(), P(), P(), P(None, ('dp', 'ep'), None),
                up_spec, up_spec, down_spec)

    def body(hidden, k_cache, v_cache, cache_len, w_q, w_k, w_v, w_o, w_router, expert_ids, w_one, w_three, w_two):
        layers = w_q.shape[0]
        k = k_cache.reshape(layers, T, ROWS, HD)
        v = v_cache.reshape(layers, T, ROWS, HD)
        id_t = jnp.swapaxes(expert_ids, 1, 2)
        for layer in range(layers):
            a_all, *extra = attention(layer, hidden, cache_len, id_t if layer == 0 else None, k, v, w_q, w_k, w_v, w_o, 2 * layer)
            if layer == 0:
                ids_t, meta, pos_t = extra
                ids, pos = jnp.swapaxes(ids_t, 1, 2), jnp.swapaxes(pos_t, 1, 2)
            mine0, theirs0 = experts(layer, 0, a_all, meta, pos_t, w_one, w_three, w_two)
            far0 = lax.ppermute(theirs0, 'pool', [(0, 1), (1, 0)])
            mine1, theirs1 = experts(layer, 1, a_all, meta, pos_t, w_one, w_three, w_two)
            hidden = merge(layer, a_all, ids, pos, mine0, far0, mine1, theirs1, w_router, 2 * layer + 1)
        return hidden

    return jax.shard_map(body, mesh=mesh, in_specs=in_specs, out_specs=tok_spec, check_vma=False)
```

profile of v0, /device:TPU:0, one launch (start us, length us, event | category | flops | bytes accessed | tf_op | source)
XLA Modules:
  0.0 204.0 jit_solution(14334285833708326065)
XLA Ops:
  0.0 33.7 %attn_0.1 = (bf16[512,896]{1,0:T(8,128)(2,1)}, s32[2,8,512]{2,1,0:T(8,128)}, s32[2,8,128]{2,1,0:T(8,128)}, s32[2,16,512]{2,1,0:T(8,128)}) custom-call(bf16[128,896]{1,0:T(8,128)(2,1)} %refs_0_.1, s32[128]{0:T(128)} %refs_1_.3, s32[2,8,128]{2,1,0:T(8,128)} %bitcast.13, bf16[2,128,512,128]{3,2,1,0:T(8,128)(2,1)} %bitcast.9, ...), custom_call_target="tpu_custom_call" | custom-call | tf_op jit(solution)/shard_map/attn_0/pallas_call | solution.py:292
  33.7 1.2 copy-done.1
  34.9 0.8 copy-done.6
  35.7 0.7 copy-done.11
  36.4 12.4 %experts_0_0.1 = (f32[1792,128]{1,0:T(8,128)S(1)}, f32[1792,128]{1,0:T(8,128)}) custom-call(bf16[512,896]{1,0:T(8,128)(2,1)S(1)} %copy-done.1, s32[2,8,128]{2,1,0:T(8,128)S(1)} %copy-done.11, s32[2,16,512]{2,1,0:T(8,128)S(1)} %copy-done.6, bf16[2,64,896,128]{3,2,1,0:T(8,128)(2,1)} %w1_ref.7, bf16[2,64,896,128]{3,2,1,0:T(8,128)(2,1)} %w3_ref.7, ...), custom_call_target="tpu_custom_call" | custom-call | flops 4000000000 | bytes 22000000 | tf_op jit(solution)/shard_map/experts_0_0/pallas_call | solution.py:406
  48.8 0.9 copy-done.8
  49.7 0.7 collective-permute-start
  50.5 0.2 copy.15
  50.7 1.0 copy.14
  51.7 0.0 copy-done.12
  51.7 0.0 copy-start.9
  51.7 19.7 %experts_0_1.1 = (f32[1792,128]{1,0:T(8,128)S(1)}, f32[1792,128]{1,0:T(8,128)S(1)}) custom-call(bf16[512,896]{1,0:T(8,128)(2,1)S(1)} %copy-done.2, s32[2,8,128]{2,1,0:T(8,128)S(1)} %copy-done.12, s32[2,16,512]{2,1,0:T(8,128)S(1)} %copy-done.7, bf16[2,64,896,128]{3,2,1,0:T(8,128)(2,1)} %w1_ref.7, bf16[2,64,896,128]{3,2,1,0:T(8,128)(2,1)} %w3_ref.7, ...), custom_call_target="tpu_custom_call" | custom-call | flops 4000000000 | bytes 22000000 | tf_op jit(solution)/shard_map/experts_0_1/pallas_call | solution.py:406
  71.4 1.0 collective-permute-done.far0_ref
  72.4 31.9 %merge_0.1.refs_0_ = bf16[128,896]{1,0:T(8,128)(2,1)S(1)} custom-call(bf16[512,896]{1,0:T(8,128)(2,1)S(1)} %copy-done.2, s32[2,512,8]{2,1,0:T(8,128)S(1)} %bitcast.7, s32[2,512,16]{2,1,0:T(8,128)S(1)} %bitcast.5, f32[1792,128]{1,0:T(8,128)S(1)} %copy-done.9, f32[1792,128]{1,0:T(8,128)} %collective-permute-done.far0_ref, ...), custom_call_target="tpu_custom_call" | custom-call | tf_op jit(solution)/shard_map/merge_0/pallas_call | solution.py:525
  104.3 0.0 copy-start.10
  104.3 0.7 copy-done.10
  105.0 31.2 %attn_1.1.a_ref = bf16[512,896]{1,0:T(8,128)(2,1)} custom-call(bf16[128,896]{1,0:T(8,128)(2,1)} %copy-done.10, s32[128]{0:T(128)} %refs_1_.3, bf16[2,128,512,128]{3,2,1,0:T(8,128)(2,1)} %bitcast.10, bf16[2,128,512,128]{3,2,1,0:T(8,128)(2,1)} %bitcast.12, bf16[2,896,2048]{2,1,0:T(8,128)(2,1)} %refs_4_.1, bf16[2,896,256]{2,1,0:T(8,128)(2,1)} %refs_5_.3, ...), custom_call_target="tpu_custom_call" | custom-call | tf_op jit(solution)/shard_map/attn_1/pallas_call | solution.py:292
  136.2 1.2 copy-done
  137.4 11.3 %experts_1_0.1 = (f32[1792,128]{1,0:T(8,128)S(1)}, f32[1792,128]{1,0:T(8,128)S(1)}) custom-call(bf16[512,896]{1,0:T(8,128)(2,1)S(1)} %copy-done, s32[2,8,128]{2,1,0:T(8,128)S(1)} %copy-done.12, s32[2,16,512]{2,1,0:T(8,128)S(1)} %copy-done.7, bf16[2,64,896,128]{3,2,1,0:T(8,128)(2,1)} %w1_ref.7, bf16[2,64,896,128]{3,2,1,0:T(8,128)(2,1)} %w3_ref.7, ...), custom_call_target="tpu_custom_call" | custom-call | flops 4000000000 | bytes 22000000 | tf_op jit(solution)/shard_map/experts_1_0/pallas_call | solution.py:406
  148.7 0.8 collective-permute-start.1
  149.5 20.1 %experts_1_1.1 = (f32[1792,128]{1,0:T(8,128)S(1)}, f32[1792,128]{1,0:T(8,128)S(1)}) custom-call(bf16[512,896]{1,0:T(8,128)(2,1)S(1)} %copy-done, s32[2,8,128]{2,1,0:T(8,128)S(1)} %copy-done.12, s32[2,16,512]{2,1,0:T(8,128)S(1)} %copy-done.7, bf16[2,64,896,128]{3,2,1,0:T(8,128)(2,1)} %w1_ref.7, bf16[2,64,896,128]{3,2,1,0:T(8,128)(2,1)} %w3_ref.7, ...), custom_call_target="tpu_custom_call" | custom-call | flops 4000000000 | bytes 22000000 | tf_op jit(solution)/shard_map/experts_1_1/pallas_call | solution.py:406
  169.6 1.7 collective-permute-done.1.far0_ref
  171.4 32.0 %merge_1.1 = bf16[128,896]{1,0:T(8,128)(2,1)S(1)} custom-call(bf16[512,896]{1,0:T(8,128)(2,1)S(1)} %copy-done, s32[2,512,8]{2,1,0:T(8,128)S(1)} %bitcast.8, s32[2,512,16]{2,1,0:T(8,128)S(1)} %bitcast.6, f32[1792,128]{1,0:T(8,128)S(1)} %get-tuple-element.25.mine0_ref, f32[1792,128]{1,0:T(8,128)S(1)} %collective-permute-done.1.far0_ref, ...), custom_call_target="tpu_custom_call" | custom-call | tf_op jit(solution)/shard_map/merge_1/pallas_call | solution.py:525
  203.3 0.7 copy.17
  (19 shorter events, 0.0 us)
Async XLA Ops:
  33.7 1.2 copy-start.1
  34.9 0.8 copy-start.6
  35.7 0.7 copy-start.11
  36.4 14.0 %copy-start.7 = (s32[2,16,512]{2,1,0:T(8,128)S(1)}, s32[2,16,512]{2,1,0:T(8,128)}, u32[]{:S(2)}) copy-start(s32[2,16,512]{2,1,0:T(8,128)} %get-tuple-element.19.pos_ref) | copy-start | bytes 196612
  36.4 14.2 %copy-start.13 = (s32[2,8,512]{2,1,0:T(8,128)S(1)}, s32[2,8,512]{2,1,0:T(8,128)}, u32[]{:S(2)}) copy-start(s32[2,8,512]{2,1,0:T(8,128)} %get-tuple-element.18) | copy-start | bytes 98308
  36.4 15.2 %copy-start.2 = (bf16[512,896]{1,0:T(8,128)(2,1)S(1)}, bf16[512,896]{1,0:T(8,128)(2,1)}, u32[]{:S(2)}) copy-start(bf16[512,896]{1,0:T(8,128)(2,1)} %get-tuple-element.17.a_ref) | copy-start | bytes 2752516
  36.4 15.2 %copy-start.12 = (s32[2,8,128]{2,1,0:T(8,128)S(1)}, s32[2,8,128]{2,1,0:T(8,128)}, u32[]{:S(2)}) copy-start(s32[2,8,128]{2,1,0:T(8,128)} %get-tuple-element.20.meta) | copy-start | bytes 24580
  48.8 0.9 copy-start.8
  49.7 22.6 %collective-permute-start = (f32[1792,128]{1,0:T(8,128)}, f32[1792,128]{1,0:T(8,128)}, u32[]{:S(2)}, u32[]{:S(2)}) collective-permute-start(f32[1792,128]{1,0:T(8,128)} %get-tuple-element.22), channel_id=1, source_target_pairs={{0,4},{4,0},{1,5},{5,1},{2,6},{6,2},{3,7},{7,3}} | collective-permute-start | bytes 2752520 | tf_op jit(solution)/shard_map/ppermute | solution.py:561
  51.7 20.7 %copy-start.3 = (f32[2,896,256]{2,1,0:T(8,128)S(1)}, f32[2,896,256]{2,1,0:T(8,128)}, u32[]{:S(2)}) copy-start(f32[2,896,256]{2,1,0:T(8,128)} %wr_ref.3) | copy-start | bytes 5505028
  51.7 20.7 %copy-start.4 = (s32[2,8,512]{1,2,0:T(8,128)S(1)}, s32[2,8,512]{1,2,0:T(8,128)}, u32[]{:S(2)}) copy-start(s32[2,8,512]{1,2,0:T(8,128)} %copy.14) | copy-start | bytes 98308
  51.7 20.7 %copy-start.9 = (f32[1792,128]{1,0:T(8,128)S(1)}, f32[1792,128]{1,0:T(8,128)}, u32[]{:S(2)}) copy-start(f32[1792,128]{1,0:T(8,128)} %copy-done.8) | copy-start | bytes 2752516
  104.3 0.7 copy-start.10
  136.2 1.2 copy-start
  148.7 22.7 %copy-start.5 = (s32[2,8,512]{1,2,0:T(8,128)S(1)}, s32[2,8,512]{1,2,0:T(8,128)}, u32[]{:S(2)}) copy-start(s32[2,8,512]{1,2,0:T(8,128)} %copy.14) | copy-start | bytes 98308
  148.7 22.7 %collective-permute-start.1 = (f32[1792,128]{1,0:T(8,128)S(1)}, f32[1792,128]{1,0:T(8,128)S(1)}, u32[]{:S(2)}, u32[]{:S(2)}) collective-permute-start(f32[1792,128]{1,0:T(8,128)S(1)} %get-tuple-element.26), channel_id=1, source_target_pairs={{0,4},{4,0},{1,5},{5,1},{2,6},{6,2},{3,7},{7,3}} | collective-permute-start | bytes 2752520 | tf_op jit(solution)/shard_map/ppermute | solution.py:561
where the time goes:
time: 204 us
  Pallas kernels  192 us (94%)
  local copies, waits for them, and re-layouts  7.39 us (4%)
  waiting for transfers between devices  2.7 us (1%)
    pallas_call x2, Pallas kernels, attention(): pl.pallas_call(functools.partial(attn_kernel, layer, first), name=f'attn_...  64.9 us
    pallas_call x2, Pallas kernels, merge(): pl.pallas_call(functools.partial(merge_kernel, layer), name=f'merge_{laye...  63.8 us
    pallas_call x4, Pallas kernels, experts(): pl.pallas_call(functools.partial(expert_kernel, layer, part), name=f'expe...  63.5 us
    unnamed x29, local copies, waits for them, and re-layouts  6.21 us
  transfers between devices with their start and end apart: 2, of which 2 were waited for; matrix products, arithmetic and copies ran while one was open for 1% of the time, Pallas kernels for 20%

commit v1 on v0

--- a/solution.py
+++ b/solution.py
@@ -104,14 +104,11 @@
             pos[base + k:base + k + 1, :] = (found - 1.0).astype(I32)
 
 
-def attn_kernel(layer, first, *refs):
-    if first:
-        (x_ref, len_ref, idt_ref, k_ref, v_ref, wq_ref, wk_ref, wv_ref, wo_ref, a_ref, ida_ref, meta_ref, pos_ref, *scr) = refs
-    else:
-        (x_ref, len_ref, k_ref, v_ref, wq_ref, wk_ref, wv_ref, wo_ref, a_ref, *scr) = refs
+def attn_steps(layer, nb, devs, len_ref, hbm, scr):
+    k_ref, v_ref, wq_ref, wk_ref, wv_ref, wo_ref = hbm
     (kbuf, vbuf, wq_v, wk_v, wv_v, wo_v, q2d, kn2d, vn2d, num, nrec, stat, ssend, srec,
-     kv_sem, w_sem, ns_sem, nr_sem, ss_sem, sr_sem, gs_sem, gr_sem, is_sem, ir_sem) = scr
-    p, e, e_x, e_d, e_z, dev_y, dev_x, dev_d, dev_z, dev_yx = peers()
+     kv_sem, w_sem, ns_sem, nr_sem, ss_sem, sr_sem, gs_sem, gr_sem) = scr
+    p, e, e_x, e_d, e_z, dev_y, dev_x, dev_d, dev_z, dev_yx = devs
 
     def tok_of(c):
         first_half = (1 - p) * HALF + c * CH
@@ -119,195 +116,209 @@
         return pl.multiple_of(jnp.where(c < NCH // 2, first_half, second_half), CH)
 
     def kv_copies(c):
-        slot = c & (NB - 1)
+        slot = c & (nb - 1)
         src = pl.ds(tok_of(c), CH)
         return (pltpu.make_async_copy(k_ref.at[layer, src], kbuf.at[slot], kv_sem.at[0, slot]),
                 pltpu.make_async_copy(v_ref.at[layer, src], vbuf.at[slot], kv_sem.at[1, slot]))
 
     weights = [pltpu.make_async_copy(r.at[layer], b, w_sem.at[i])
                for i, (r, b) in enumerate(((wq_ref, wq_v), (wk_ref, wk_v), (wv_ref, wv_v), (wo_ref, wo_v)))]
-    for cp in weights[:3]:
-        cp.start()
-    for c in range(2):
-        for cp in kv_copies(jnp.int32(c)):
+    def start_kv(first, last):
+        for c in range(first, last):
+            for cp in kv_copies(jnp.int32(c)):
+                cp.start()
+
+    def start(chunks):
+        for cp in weights[:3]:
             cp.start()
-
+        start_kv(0, chunks)
+
+    def run(x_ref, a_ref, started, between):
+        normed = rms(x_ref[...]).astype(BF16)
+        for cp in weights[:3]:
+            cp.wait()
+        start_kv(started, nb)
+        weights[3].start()
+        for hp in range(H // 2):
+            pair = mm(normed, wq_v[:, hp * 256:(hp + 1) * 256]).astype(BF16).astype(F32)
+            for i in range(2):
+                q2d[pl.ds(hp * 2 + i, T, stride=H), :] = pair[:, i * HD:(i + 1) * HD]
+        for w, dst in ((wk_v, kn2d), (wv_v, vn2d)):
+            pair = mm(normed, w[...]).astype(BF16).astype(F32)
+            for i in range(KV):
+                dst[pl.ds(i, T, stride=KV), :] = pair[:, i * HD:(i + 1) * HD]
+
+        scale = HD ** -0.5
+        col = iota((H, ROWS), 1)
+        group_ok = (col & 1) == (iota((H, ROWS), 0) // (H // KV))
+        col_pos = jnp.where(group_ok, col >> 1, 1 << 30)
+        lane = iota((H, T), 1)
+
+        def heads_of(ref, tok):
+            two = ref[pl.ds(tok * KV, KV), :]
+            return jnp.concatenate([jnp.broadcast_to(two[i:i + 1], (H // KV, HD)) for i in range(KV)], axis=0)
+
+        def num_copy(c):
+            rows = pl.ds(pl.multiple_of(c * (CH * H), CH * H), CH * H)
+            return remote(num.at[rows], nrec.at[rows], ns_sem.at[c], nr_sem.at[c], dev_y)
+
+        stat_copy = remote(ssend, srec, ss_sem, sr_sem, dev_y)
+
+        def chunk(c, carry):
+            slot = c & (nb - 1)
+            for cp in kv_copies(c):
+                cp.wait()
+            tok0 = tok_of(c)
+            m_all, l_all, n_all = stat[0], stat[1], stat[2]
+            for j0 in range(0, CH, 4):
+                group = range(j0, j0 + 4)
+                qs, ss = {}, {}
+                for j in group:
+                    qs[j] = q2d[pl.ds(pl.multiple_of((tok0 + j) * H, H), H), :]
+                    ss[j] = lax.dot_general(qs[j].astype(BF16), kbuf[slot, j], (((1,), (1,)), ((), ())),
+                                            preferred_element_type=F32) * scale
+                ps = {}
+                for j in group:
+                    limit = len_ref[tok0 + j] - p * POS
+                    s = jnp.where(col_pos < limit, ss[j], -1e30)
+                    s_new = jnp.sum(qs[j] * heads_of(kn2d, tok0 + j), axis=1, keepdims=True) * scale
+                    m = jnp.maximum(jnp.max(s, axis=1, keepdims=True), s_new)
+                    pr = jnp.exp(s - m)
+                    ps[j] = pr.astype(BF16)
+                    here = lane == c * CH + j
+                    m_all = jnp.where(here, m, m_all)
+                    l_all = jnp.where(here, jnp.sum(pr, axis=1, keepdims=True), l_all)
+                    n_all = jnp.where(here, s_new, n_all)
+                for j in group:
+                    num[pl.ds(pl.multiple_of((c * CH + j) * H, H), H), :] = mm(ps[j], vbuf[slot, j])
+            stat[0], stat[1], stat[2] = m_all, l_all, n_all
+
+            @pl.when(c + nb < NCH)
+            def _():
+                for cp in kv_copies(c + nb):
+                    cp.start()
+
+            @pl.when(c == NCH // 2 - 1)
+            def _():
+                ssend[0], ssend[1] = m_all, l_all
+
+            @pl.when((c >= 1) & (c <= NCH // 2))
+            def _():
+                num_copy(c - 1).start()
+
+            @pl.when(c == NCH // 2)
+            def _():
+                stat_copy.start()
+
+            return carry
+
+        stat[...] = jnp.zeros_like(stat)
+        lax.fori_loop(0, NCH, chunk, 0)
+
+        weights[3].wait()
+        stat_copy.wait()
+        m_own, l_own, s_new = stat[0], stat[1], stat[2]
+        m_far = pltpu.roll(srec[0], HALF, axis=1)
+        l_far = pltpu.roll(srec[1], HALF, axis=1)
+        m = jnp.maximum(m_own, m_far)
+        w_own, w_far, w_new = jnp.exp(m_own - m), jnp.exp(m_far - m), jnp.exp(s_new - m)
+        denom = l_own * w_own + l_far * w_far + w_new
+        c_own, c_far, c_new = w_own / denom, w_far / denom, w_new / denom
+
+        def combine(c, carry):
+            num_copy(c).wait()
+            for j in range(CH):
+                i = c * CH + j
+                pick = lane == HALF + i
+                own, far, new = [jnp.sum(jnp.where(pick, v, 0.0), axis=1, keepdims=True) for v in (c_own, c_far, c_new)]
+                there = pl.ds(pl.multiple_of(i * H, H), H)
+                here = pl.ds(pl.multiple_of((HALF + i) * H, H), H)
+                num[here, :] = num[here, :] * own + nrec[there, :] * far + heads_of(vn2d, p * HALF + i) * new
+            return carry
+
+        lax.fori_loop(0, NCH // 2, combine, 0)
+
+        proj = jnp.zeros((HALF, D), F32)
+        for hp in range(H // 2):
+            pair = jnp.concatenate([num[pl.ds(HALF * H + hp * 2 + i, HALF, stride=H), :].astype(BF16) for i in range(2)], axis=1)
+            proj = proj + mm(pair, wo_v[hp * 256:(hp + 1) * 256, :])
+        mine = pl.ds(pl.multiple_of(p * HALF, HALF), HALF)
+
+        def rows(pp, ee):
+            return pl.ds(pl.multiple_of(ee * T + pp * HALF, HALF), HALF)
+
+        a_ref[rows(p, e), :] = (x_ref[mine, :].astype(F32) + proj).astype(BF16)
+
+        def gather(i, pp, ee, dev):
+            block = a_ref.at[rows(pp, ee)]
+            cp = remote(block, block, gs_sem.at[i], gr_sem.at[i], dev)
+            cp.start()
+            return cp
+
+        copies = [gather(0, p, e, dev_yx), gather(1, p, e, dev_x), gather(2, p, e, dev_y), gather(3, p, e, dev_d)]
+        between()
+        for i, pp, ee in ((2, 1 - p, e), (1, p, e_x), (0, 1 - p, e_x)):
+            copies[i].wait_recv()
+            copies.append(gather(len(copies), pp, ee, dev_d))
+        for i in range(3, 7):
+            copies[i].wait_recv()
+        for cp in copies:
+            cp.wait_send()
+
+    return start, run
+
+
+def attn_kernel(x_ref, len_ref, idt_ref, *refs):
+    hbm, (a_ref, ida_ref, meta_ref, pos_ref), scr = refs[:6], refs[6:10], refs[10:]
+    is_sem, ir_sem = scr[-2:]
+    devs = peers()
+    p, e, e_x, e_d, e_z, dev_y, dev_x, dev_d, dev_z, dev_yx = devs
+    start, run = attn_steps(0, NB, devs, len_ref, hbm, scr[:-2])
+    start(2)
     entry_barrier((dev_y, dev_x, dev_d, dev_z, dev_yx))
-
+    mine = (slice(None), slice(None), pl.ds(pl.multiple_of(e * T, T), T))
+    ida_ref[mine] = idt_ref[...]
     id_copies = []
-    if first:
-        mine = (slice(None), slice(None), pl.ds(pl.multiple_of(e * T, T), T))
-        ida_ref[mine] = idt_ref[...]
-        for i, dev in enumerate((dev_x, dev_d, dev_z)):
-            id_copies.append(remote(idt_ref, ida_ref.at[mine], is_sem.at[i], ir_sem.at[i], dev))
-            id_copies[-1].start()
-
-    normed = rms(x_ref[...]).astype(BF16)
-    for cp in weights[:3]:
-        cp.wait()
-    for c in range(2, NB):
-        for cp in kv_copies(jnp.int32(c)):
-            cp.start()
-    weights[3].start()
-    for hp in range(H // 2):
-        pair = mm(normed, wq_v[:, hp * 256:(hp + 1) * 256]).astype(BF16).astype(F32)
-        for i in range(2):
-            q2d[pl.ds(hp * 2 + i, T, stride=H), :] = pair[:, i * HD:(i + 1) * HD]
-    for w, dst in ((wk_v, kn2d), (wv_v, vn2d)):
-        pair = mm(normed, w[...]).astype(BF16).astype(F32)
-        for i in range(KV):
-            dst[pl.ds(i, T, stride=KV), :] = pair[:, i * HD:(i + 1) * HD]
-
-    scale = HD ** -0.5
-    col = iota((H, ROWS), 1)
-    group_ok = (col & 1) == (iota((H, ROWS), 0) // (H // KV))
-    col_pos = jnp.where(group_ok, col >> 1, 1 << 30)
-    lane = iota((H, T), 1)
-
-    def heads_of(ref, tok):
-        two = ref[pl.ds(tok * KV, KV), :]
-        return jnp.concatenate([jnp.broadcast_to(two[i:i + 1], (H // KV, HD)) for i in range(KV)], axis=0)
-
-    def num_copy(c):
-        rows = pl.ds(pl.multiple_of(c * (CH * H), CH * H), CH * H)
-        return remote(num.at[rows], nrec.at[rows], ns_sem.at[c], nr_sem.at[c], dev_y)
-
-    stat_copy = remote(ssend, srec, ss_sem, sr_sem, dev_y)
-
-    def chunk(c, carry):
-        slot = c & (NB - 1)
-        for cp in kv_copies(c):
-            cp.wait()
-        tok0 = tok_of(c)
-        m_all, l_all, n_all = stat[0], stat[1], stat[2]
-        for j0 in range(0, CH, 4):
-            group = range(j0, j0 + 4)
-            qs, ss = {}, {}
-            for j in group:
-                qs[j] = q2d[pl.ds(pl.multiple_of((tok0 + j) * H, H), H), :]
-                ss[j] = lax.dot_general(qs[j].astype(BF16), kbuf[slot, j], (((1,), (1,)), ((), ())),
-                                        preferred_element_type=F32) * scale
-            ps = {}
-            for j in group:
-                limit = len_ref[tok0 + j] - p * POS
-                s = jnp.where(col_pos < limit, ss[j], -1e30)
-                s_new = jnp.sum(qs[j] * heads_of(kn2d, tok0 + j), axis=1, keepdims=True) * scale
-                m = jnp.maximum(jnp.max(s, axis=1, keepdims=True), s_new)
-                pr = jnp.exp(s - m)
-                ps[j] = pr.astype(BF16)
-                here = lane == c * CH + j
-                m_all = jnp.where(here, m, m_all)
-                l_all = jnp.where(here, jnp.sum(pr, axis=1, keepdims=True), l_all)
-                n_all = jnp.where(here, s_new, n_all)
-            for j in group:
-                num[pl.ds(pl.multiple_of((c * CH + j) * H, H), H), :] = mm(ps[j], vbuf[slot, j])
-        stat[0], stat[1], stat[2] = m_all, l_all, n_all
-
-        @pl.when(c + NB < NCH)
-        def _():
-            for cp in kv_copies(c + NB):
-                cp.start()
-
-        @pl.when(c == NCH // 2 - 1)
-        def _():
-            ssend[0], ssend[1] = m_all, l_all
-
-        @pl.when((c >= 1) & (c <= NCH // 2))
-        def _():
-            num_copy(c - 1).start()
-
-        @pl.when(c == NCH // 2)
-        def _():
-            stat_copy.start()
-
-        return carry
-
-    stat[...] = jnp.zeros_like(stat)
-    lax.fori_loop(0, NCH, chunk, 0)
-
-    weights[3].wait()
-    stat_copy.wait()
-    m_own, l_own, s_new = stat[0], stat[1], stat[2]
-    m_far = pltpu.roll(srec[0], HALF, axis=1)
-    l_far = pltpu.roll(srec[1], HALF, axis=1)
-    m = jnp.maximum(m_own, m_far)
-    w_own, w_far, w_new = jnp.exp(m_own - m), jnp.exp(m_far - m), jnp.exp(s_new - m)
-    denom = l_own * w_own + l_far * w_far + w_new
-    c_own, c_far, c_new = w_own / denom, w_far / denom, w_new / denom
-
-    def combine(c, carry):
-        num_copy(c).wait()
-        for j in range(CH):
-            i = c * CH + j
-            pick = lane == HALF + i
-            own, far, new = [jnp.sum(jnp.where(pick, v, 0.0), axis=1, keepdims=True) for v in (c_own, c_far, c_new)]
-            there = pl.ds(pl.multiple_of(i * H, H), H)
-            here = pl.ds(pl.multiple_of((HALF + i) * H, H), H)
-            num[here, :] = num[here, :] * own + nrec[there, :] * far + heads_of(vn2d, p * HALF + i) * new
-        return carry
-
-    lax.fori_loop(0, NCH // 2, combine, 0)
-
-    proj = jnp.zeros((HALF, D), F32)
-    for hp in range(H // 2):
-        pair = jnp.concatenate([num[pl.ds(HALF * H + hp * 2 + i, HALF, stride=H), :].astype(BF16) for i in range(2)], axis=1)
-        proj = proj + mm(pair, wo_v[hp * 256:(hp + 1) * 256, :])
-    mine = pl.ds(pl.multiple_of(p * HALF, HALF), HALF)
-
-    def rows(pp, ee):
-        return pl.ds(pl.multiple_of(ee * T + pp * HALF, HALF), HALF)
-
-    a_ref[rows(p, e), :] = (x_ref[mine, :].astype(F32) + proj).astype(BF16)
-
-    def gather(i, pp, ee, dev):
-        block = a_ref.at[rows(pp, ee)]
-        cp = remote(block, block, gs_sem.at[i], gr_sem.at[i], dev)
-        cp.start()
-        return cp
-
-    copies = [gather(0, p, e, dev_yx), gather(1, p, e, dev_x), gather(2, p, e, dev_y), gather(3, p, e, dev_d)]
-    if first:
+    for i, dev in enumerate((dev_x, dev_d, dev_z)):
+        id_copies.append(remote(idt_ref, ida_ref.at[mine], is_sem.at[i], ir_sem.at[i], dev))
+        id_copies[-1].start()
+
+    def make_tables():
         for cp in id_copies:
             cp.wait()
         for n in range(ida_ref.shape[0]):
             route(ida_ref.at[n], e, meta_ref.at[n], pos_ref.at[n])
-    for i, pp, ee in ((2, 1 - p, e), (1, p, e_x), (0, 1 - p, e_x)):
-        copies[i].wait_recv()
-        copies.append(gather(len(copies), pp, ee, dev_d))
-    for i in range(3, 7):
-        copies[i].wait_recv()
-    for cp in copies:
-        cp.wait_send()
-
-
-def attention(layer, x, cache_len, id_t, k, v, wq, wk, wv, wo, cid):
-    first = id_t is not None
+
+    run(x_ref, a_ref, 2, make_tables)
+
+
+def attn_scratch(nb):
+    dma = pltpu.SemaphoreType.DMA
+    return [
+        pltpu.VMEM((nb, CH, ROWS, HD), BF16), pltpu.VMEM((nb, CH, ROWS, HD), BF16),
+        pltpu.VMEM((D, H * HD), BF16), pltpu.VMEM((D, KV * HD), BF16), pltpu.VMEM((D, KV * HD), BF16),
+        pltpu.VMEM((H * HD, D), BF16),
+        pltpu.VMEM((T * H, HD), F32), pltpu.VMEM((T * KV, HD), F32), pltpu.VMEM((T * KV, HD), F32),
+        pltpu.VMEM((T * H, HD), F32), pltpu.VMEM((HALF * H, HD), F32),
+        pltpu.VMEM((3, H, T), F32), pltpu.VMEM((2, H, T), F32), pltpu.VMEM((2, H, T), F32),
+        dma((2, nb)), dma((4,)), dma((NCH // 2,)), dma((NCH // 2,)), dma(()), dma(()), dma((7,)), dma((7,)),
+    ]
+
+
+def attention(x, cache_len, id_t, hbm):
     vm, sm, hb = (pl.BlockSpec(memory_space=m) for m in (pltpu.VMEM, pltpu.SMEM, pltpu.HBM))
     dma = pltpu.SemaphoreType.DMA
-    outs = [jax.ShapeDtypeStruct((ALL, D), BF16)]
-    if first:
-        layers = id_t.shape[0]
-        outs += [jax.ShapeDtypeStruct((layers, 8, ALL), I32), jax.ShapeDtypeStruct((layers, 8, 128), I32),
-                 jax.ShapeDtypeStruct((layers, 16, ALL), I32)]
-    out = pl.pallas_call(
-        functools.partial(attn_kernel, layer, first),
-        name=f"attn_{layer}",
-        out_shape=outs,
-        in_specs=[vm, sm] + ([vm] if first else []) + [hb] * 6,
-        out_specs=[vm] * len(outs),
-        scratch_shapes=[
-            pltpu.VMEM((NB, CH, ROWS, HD), BF16), pltpu.VMEM((NB, CH, ROWS, HD), BF16),
-            pltpu.VMEM((D, H * HD), BF16), pltpu.VMEM((D, KV * HD), BF16), pltpu.VMEM((D, KV * HD), BF16),
-            pltpu.VMEM((H * HD, D), BF16),
-            pltpu.VMEM((T * H, HD), F32), pltpu.VMEM((T * KV, HD), F32), pltpu.VMEM((T * KV, HD), F32),
-            pltpu.VMEM((T * H, HD), F32), pltpu.VMEM((HALF * H, HD), F32),
-            pltpu.VMEM((3, H, T), F32), pltpu.VMEM((2, H, T), F32), pltpu.VMEM((2, H, T), F32),
-            dma((2, NB)), dma((4,)), dma((NCH // 2,)), dma((NCH // 2,)), dma(()), dma(()),
-            dma((7,)), dma((7,)), dma((3,)), dma((3,)),
-        ],
-        compiler_params=pltpu.CompilerParams(collective_id=cid, has_side_effects=True, vmem_limit_bytes=61 * MIB),
-    )(*([x, cache_len] + ([id_t] if first else []) + [k, v, wq, wk, wv, wo]))
-    return out
+    layers = id_t.shape[0]
+    return pl.pallas_call(
+        attn_kernel,
+        name="attn_0",
+        out_shape=[jax.ShapeDtypeStruct((ALL, D), BF16), jax.ShapeDtypeStruct((layers, 8, ALL), I32),
+                   jax.ShapeDtypeStruct((layers, 8, 128), I32), jax.ShapeDtypeStruct((layers, 16, ALL), I32)],
+        in_specs=[vm, sm, vm] + [hb] * 6,
+        out_specs=[vm] * 4,
+        scratch_shapes=attn_scratch(NB) + [dma((3,)), dma((3,))],
+        compiler_params=pltpu.CompilerParams(collective_id=0, has_side_effects=True, vmem_limit_bytes=61 * MIB),
+    )(x, cache_len, id_t, *hbm)
 
 
 def expert_kernel(layer, part, a_ref, meta, pos_ref, w1_ref, w3_ref, w2_ref, mine_ref, theirs_ref,
@@ -421,21 +432,23 @@
     )(a_all, meta, pos, w1, w3, w2)
 
 
-def merge_kernel(layer, a_ref, id_ref, pos_ref, mine0_ref, far0_ref, mine1_ref, theirs1_ref, wr_ref, x_ref,
-                 y_own, y_far, wr, gate, base, acc, back, xsend, xfar,
-                 l_sem, ys_sem, yr_sem, bs_sem, br_sem, fs_sem, fr_sem):
-    p, e, e_x, e_d, e_z, dev_y, dev_x, dev_d, dev_z, dev_yx = peers()
+def merge_steps(layer, devs, ins, x_ref, scr, beside):
+    a_ref, id_ref, pos_ref, mine0_ref, far0_ref, mine1_ref, theirs1_ref, wr_ref = ins
+    (y_own, y_far, wr, gate, base, acc, back, xsend, xfar,
+     l_sem, ys_sem, yr_sem, bs_sem, br_sem, fs_sem, fr_sem) = scr
+    p, e, e_x, e_d, e_z, dev_y, dev_x, dev_d, dev_z, dev_yx = devs
     loads = [pltpu.make_async_copy(src, dst, l_sem.at[i])
              for i, (src, dst) in enumerate(((wr_ref.at[layer], wr), (mine0_ref, y_own.at[0]), (far0_ref, y_far.at[0]),
                                              (mine1_ref, y_own.at[1])))]
     for cp in loads:
         cp.start()
-    entry_barrier((dev_y, dev_x, dev_d, dev_z))
+    entry_barrier((dev_y, dev_x, dev_d, dev_z, dev_yx))
     spans = [(t * NR, NR) for t in range(3)] + [(3 * NR, NR // 2)]
     y_copies = [remote(theirs1_ref.at[pl.ds(b, n)], y_far.at[1, pl.ds(b, n)], ys_sem.at[t], yr_sem.at[t], dev_y)
                 for t, (b, n) in enumerate(spans)]
     for cp in y_copies:
         cp.start()
+    beside()
 
     loads[0].wait()
     u = rms(a_ref[...]).astype(BF16)
@@ -519,24 +532,56 @@
         cp.wait_send()
 
 
-def merge(layer, a_all, ids, pos, mine0, far0, mine1, theirs1, wr, cid):
-    vm, hb, anywhere = (pl.BlockSpec(memory_space=m) for m in (pltpu.VMEM, pltpu.HBM, pl.ANY))
+MERGE_IN, MERGE_SCR = 8, 16
+
+
+def merge_last_kernel(layer, *refs):
+    merge_steps(layer, peers(), refs[:MERGE_IN], refs[MERGE_IN], refs[MERGE_IN + 1:], lambda: None)
+
+
+def merge_next_kernel(layer, *refs):
+    ins, len_ref, hbm, a_ref = refs[:MERGE_IN], refs[MERGE_IN], refs[MERGE_IN + 1:MERGE_IN + 7], refs[MERGE_IN + 7]
+    x_ref, scr = refs[MERGE_IN + 8], refs[MERGE_IN + 9:]
+    devs = peers()
+    start, run = attn_steps(layer + 1, NCH, devs, len_ref, hbm, scr[MERGE_SCR:])
+    merge_steps(layer, devs, ins, x_ref, scr[:MERGE_SCR], lambda: start(NCH))
+    run(x_ref, a_ref, NCH, lambda: None)
+
+
+def merge_scratch():
     dma = pltpu.SemaphoreType.DMA
+    return [
+        pltpu.VMEM((2, PR, 128), F32), pltpu.VMEM((2, PR, 128), F32),
+        pltpu.VMEM((D, 256), F32), pltpu.VMEM((3, ALL, PAIRS), BF16),
+        pltpu.VMEM((4, ALL, 128), F32), pltpu.VMEM((4, ALL, 128), F32), pltpu.VMEM((4, 3, T, 128), F32),
+        pltpu.VMEM((4, T, 128), BF16), pltpu.VMEM((4, T, 128), BF16),
+        dma((4,)), dma((4,)), dma((4,)), dma((4, 3)), dma((4, 3)), dma((4,)), dma((4,)),
+    ]
+
+
+def merge(layer, last, ins, cache_len, hbm):
+    vm, sm, hb, anywhere = (pl.BlockSpec(memory_space=m) for m in (pltpu.VMEM, pltpu.SMEM, pltpu.HBM, pl.ANY))
+    in_specs = [vm, vm, vm, anywhere, anywhere, anywhere, anywhere, hb]
+    params = functools.partial(pltpu.CompilerParams, collective_id=1 + layer, has_side_effects=True)
+    if last:
+        return pl.pallas_call(
+            functools.partial(merge_last_kernel, layer),
+            name=f"merge_{layer}",
+            out_shape=jax.ShapeDtypeStruct((T, D), BF16),
+            in_specs=in_specs,
+            out_specs=vm,
+            scratch_shapes=merge_scratch(),
+            compiler_params=params(vmem_limit_bytes=24 * MIB),
+        )(*ins)
     return pl.pallas_call(
-        functools.partial(merge_kernel, layer),
-        name=f"merge_{layer}",
-        out_shape=jax.ShapeDtypeStruct((T, D), BF16),
-        in_specs=[vm, vm, vm, anywhere, anywhere, anywhere, anywhere, hb],
+        functools.partial(merge_next_kernel, layer),
+        name=f"merge_attn_{layer}",
+        out_shape=jax.ShapeDtypeStruct((ALL, D), BF16),
+        in_specs=in_specs + [sm] + [hb] * 6,
         out_specs=vm,
-        scratch_shapes=[
-            pltpu.VMEM((2, PR, 128), F32), pltpu.VMEM((2, PR, 128), F32),
-            pltpu.VMEM((D, 256), F32), pltpu.VMEM((3, ALL, PAIRS), BF16),
-            pltpu.VMEM((4, ALL, 128), F32), pltpu.VMEM((4, ALL, 128), F32), pltpu.VMEM((4, 3, T, 128), F32),
-            pltpu.VMEM((4, T, 128), BF16), pltpu.VMEM((4, T, 128), BF16),
-            dma((4,)), dma((4,)), dma((4,)), dma((4, 3)), dma((4, 3)), dma((4,)), dma((4,)),
-        ],
-        compiler_params=pltpu.CompilerParams(collective_id=cid, has_side_effects=True, vmem_limit_bytes=24 * MIB),
-    )(a_all, ids, pos, mine0, far0, mine1, theirs1, wr)
+        scratch_shapes=[pltpu.VMEM((T, D), BF16)] + merge_scratch() + attn_scratch(NCH),
+        compiler_params=params(vmem_limit_bytes=67043328),
+    )(*ins, cache_len, *hbm)
 
 
 def solution(mesh):
@@ -552,15 +597,16 @@
         k = k_cache.reshape(layers, T, ROWS, HD)
         v = v_cache.reshape(layers, T, ROWS, HD)
         id_t = jnp.swapaxes(expert_ids, 1, 2)
+        hbm = (k, v, w_q, w_k, w_v, w_o)
+        a_all, ids_t, meta, pos_t = attention(hidden, cache_len, id_t, hbm)
+        ids, pos = jnp.swapaxes(ids_t, 1, 2), jnp.swapaxes(pos_t, 1, 2)
         for layer in range(layers):
-            a_all, *extra = attention(layer, hidden, cache_len, id_t if layer == 0 else None, k, v, w_q, w_k, w_v, w_o, 2 * layer)
-            if layer == 0:
-                ids_t, meta, pos_t = extra
-                ids, pos = jnp.swapaxes(ids_t, 1, 2), jnp.swapaxes(pos_t, 1, 2)
             mine0, theirs0 = experts(layer, 0, a_all, meta, pos_t, w_one, w_three, w_two)
             far0 = lax.ppermute(theirs0, 'pool', [(0, 1), (1, 0)])
             mine1, theirs1 = experts(layer, 1, a_all, meta, pos_t, w_one, w_three, w_two)
-            hidden = merge(layer, a_all, ids, pos, mine0, far0, mine1, theirs1, w_router, 2 * layer + 1)
-        return hidden
+            ins = (a_all, ids, pos, mine0, far0, mine1, theirs1, w_router)
+            last = layer == layers - 1
+            a_all = merge(layer, last, ins, cache_len, hbm)
+        return a_all
 
     return jax.shard_map(body, mesh=mesh, in_specs=in_specs, out_specs=tok_spec, check_vma=False)

time: 204 us -> 206 us (level); the launches traced: 204 us -> 204 us
  local copies, waits for them, and re-layouts: 7.39 us -> 11.9 us
  waiting for transfers between devices: 2.7 us -> 0.01 us
    unnamed x29 -> x35, local copies, waits for them, and re-layouts: 6.21 us -> 9.88 us
    ppermute x2, waiting for transfers between devices: 2.7 us -> 0.01 us  [body(): far0 = lax.ppermute(theirs0, 'pool', [(0, 1), (1, 0)])]
    pallas_call x4 -> x3, Pallas kernels: 129 us -> 127 us  [the longest x1 60.6 us: merge(): pl.pallas_call(functools.partial(merge_next_kernel, layer), name=f'merge_...]
  transfers between devices with their start and end apart: 2 -> 2, of which waited for: 2 -> 0; matrix products, arithmetic and copies ran while one was open for 1% -> 1% of each run, Pallas kernels for 20% -> 20%
where the time goes in v1:
time: 206 us; the launch traced here: 204 us
  Pallas kernels  190 us (92%)
  local copies, waits for them, and re-layouts  11.9 us (6%)
    pallas_call x4, Pallas kernels, experts(): pl.pallas_call(functools.partial(expert_kernel, layer, part), name=f'expe...  63.5 us
    pallas_call x1, Pallas kernels, merge(): pl.pallas_call(functools.partial(merge_next_kernel, layer), name=f'merge_...  60.6 us
    pallas_call x1, Pallas kernels, attention(): pl.pallas_call(attn_kernel, name='attn_0', out_shape=[jax.ShapeDtypeStruc...  33.7 us
    pallas_call x1, Pallas kernels, merge(): pl.pallas_call(functools.partial(merge_last_kernel, layer), name=f'merge_...  32.4 us
    unnamed x35, local copies, waits for them, and re-layouts  9.88 us
  transfers between devices with their start and end apart: 2, of which 0 were waited for; matrix products, arithmetic and copies ran while one was open for 1% of the time, Pallas kernels for 20%

profile of v1, /device:TPU:0, one launch (start us, length us, event | category | flops | bytes accessed | tf_op | source)
XLA Modules:
  0.0 203.9 jit_solution(5026178400849533071)
XLA Ops:
  0.0 33.7 %attn_0.1 = (bf16[512,896]{1,0:T(8,128)(2,1)}, s32[2,8,512]{2,1,0:T(8,128)}, s32[2,8,128]{2,1,0:T(8,128)}, s32[2,16,512]{2,1,0:T(8,128)}) custom-call(bf16[128,896]{1,0:T(8,128)(2,1)} %x_ref.1, s32[128]{0:T(128)} %refs_8_.1, s32[2,8,128]{2,1,0:T(8,128)} %bitcast.13, bf16[2,128,512,128]{3,2,1,0:T(8,128)(2,1)} %bitcast.9, bf16[2,128,512,128]{3,2,1,0:T(8,128)(2,1)} %bitcast.11, ...), custom_call_target="tpu_custom_call" | custom-call | tf_op jit(solution)/shard_map/attn_0/pallas_call | solution.py:312
  33.7 1.2 copy-done.1
  34.9 0.8 copy-done.6
  35.7 0.7 copy-done.12
  36.4 11.4 %experts_0_0.1 = (f32[1792,128]{1,0:T(8,128)S(1)}, f32[1792,128]{1,0:T(8,128)S(1)}) custom-call(bf16[512,896]{1,0:T(8,128)(2,1)S(1)} %copy-done.1, s32[2,8,128]{2,1,0:T(8,128)S(1)} %copy-done.12, s32[2,16,512]{2,1,0:T(8,128)S(1)} %copy-done.6, bf16[2,64,896,128]{3,2,1,0:T(8,128)(2,1)} %w1_ref.7, bf16[2,64,896,128]{3,2,1,0:T(8,128)(2,1)} %w3_ref.7, ...), custom_call_target="tpu_custom_call" | custom-call | flops 4000000000 | bytes 22000000 | tf_op jit(solution)/shard_map/experts_0_0/pallas_call | solution.py:417
  47.9 1.0 copy-done.9
  48.8 0.7 collective-permute-start
  49.5 1.0 copy.15
  50.5 1.0 copy.14
  51.6 18.8 %experts_0_1.1 = (f32[1792,128]{1,0:T(8,128)S(1)}, f32[1792,128]{1,0:T(8,128)S(1)}) custom-call(bf16[512,896]{1,0:T(8,128)(2,1)S(1)} %copy-done.2, s32[2,8,128]{2,1,0:T(8,128)S(1)} %copy-done.13, s32[2,16,512]{2,1,0:T(8,128)S(1)} %copy-done.7, bf16[2,64,896,128]{3,2,1,0:T(8,128)(2,1)} %w1_ref.7, bf16[2,64,896,128]{3,2,1,0:T(8,128)(2,1)} %w3_ref.7, ...), custom_call_target="tpu_custom_call" | custom-call | flops 4000000000 | bytes 22000000 | tf_op jit(solution)/shard_map/experts_0_1/pallas_call | solution.py:417
  70.4 0.9 copy-done.10
  71.3 0.9 copy-done.11
  72.2 0.0 collective-permute-done.refs_4_
  72.2 0.9 copy-done.15
  73.1 60.6 %merge_attn_0.1.a_ref.refs_0_ = bf16[512,896]{1,0:T(8,128)(2,1)} custom-call(bf16[512,896]{1,0:T(8,128)(2,1)} %get-tuple-element.17.a_ref.refs_0_, s32[2,512,8]{2,1,0:T(8,128)} %bitcast.7, s32[2,512,16]{2,1,0:T(8,128)} %bitcast.5, f32[1792,128]{1,0:T(8,128)} %copy-done.9, f32[1792,128]{1,0:T(8,128)} %copy-done.15, f32[1792,128]{1,0:T(8,128)} %copy-done.10, ...), custom_call_target="tpu_custom_call" | custom-call | tf_op jit(solution)/shard_map/merge_attn_0/pallas_call | solution.py:576
  133.8 1.2 copy-done
  135.0 0.8 copy-done.8
  135.8 0.7 copy-done.14
  136.5 11.4 %experts_1_0.1 = (f32[1792,128]{1,0:T(8,128)S(1)}, f32[1792,128]{1,0:T(8,128)S(1)}) custom-call(bf16[512,896]{1,0:T(8,128)(2,1)S(1)} %copy-done, s32[2,8,128]{2,1,0:T(8,128)S(1)} %copy-done.14, s32[2,16,512]{2,1,0:T(8,128)S(1)} %copy-done.8, bf16[2,64,896,128]{3,2,1,0:T(8,128)(2,1)} %w1_ref.7, bf16[2,64,896,128]{3,2,1,0:T(8,128)(2,1)} %w3_ref.7, ...), custom_call_target="tpu_custom_call" | custom-call | flops 4000000000 | bytes 22000000 | tf_op jit(solution)/shard_map/experts_1_0/pallas_call | solution.py:417
  147.9 0.0 copy-start.3
  147.9 1.0 collective-permute-start.1
  148.9 21.9 %experts_1_1.1 = (f32[1792,128]{1,0:T(8,128)S(1)}, f32[1792,128]{1,0:T(8,128)S(1)}) custom-call(bf16[512,896]{1,0:T(8,128)(2,1)S(1)} %copy-done, s32[2,8,128]{2,1,0:T(8,128)S(1)} %copy-done.14, s32[2,16,512]{2,1,0:T(8,128)S(1)} %copy-done.8, bf16[2,64,896,128]{3,2,1,0:T(8,128)(2,1)} %w1_ref.7, bf16[2,64,896,128]{3,2,1,0:T(8,128)(2,1)} %w3_ref.7, ...), custom_call_target="tpu_custom_call" | custom-call | flops 4000000000 | bytes 22000000 | tf_op jit(solution)/shard_map/experts_1_1/pallas_call | solution.py:417
  170.8 32.4 %merge_1.1 = bf16[128,896]{1,0:T(8,128)(2,1)S(1)} custom-call(bf16[512,896]{1,0:T(8,128)(2,1)S(1)} %copy-done, s32[2,512,8]{2,1,0:T(8,128)S(1)} %bitcast.8, s32[2,512,16]{2,1,0:T(8,128)S(1)} %bitcast.6, f32[1792,128]{1,0:T(8,128)S(1)} %get-tuple-element.25.refs_3_, f32[1792,128]{1,0:T(8,128)S(1)} %collective-permute-done.1.refs_4_, ...), custom_call_target="tpu_custom_call" | custom-call | tf_op jit(solution)/shard_map/merge_1/pallas_call | solution.py:567
  203.3 0.7 copy.17
  (24 shorter events, 0.0 us)
Async XLA Ops:
  33.7 1.2 copy-start.1
  34.9 0.8 copy-start.6
  35.7 0.7 copy-start.12
  36.4 13.1 %copy-start.7 = (s32[2,16,512]{2,1,0:T(8,128)S(1)}, s32[2,16,512]{2,1,0:T(8,128)}, u32[]{:S(2)}) copy-start(s32[2,16,512]{2,1,0:T(8,128)} %get-tuple-element.19.pos_ref) | copy-start | bytes 196612
  36.4 14.1 %copy-start.16 = (s32[2,8,512]{2,1,0:T(8,128)S(1)}, s32[2,8,512]{2,1,0:T(8,128)}, u32[]{:S(2)}) copy-start(s32[2,8,512]{2,1,0:T(8,128)} %get-tuple-element.18) | copy-start | bytes 98308
  36.4 15.1 %copy-start.2 = (bf16[512,896]{1,0:T(8,128)(2,1)S(1)}, bf16[512,896]{1,0:T(8,128)(2,1)}, u32[]{:S(2)}) copy-start(bf16[512,896]{1,0:T(8,128)(2,1)} %get-tuple-element.17.a_ref.refs_0_) | copy-start | bytes 2752516
  36.4 15.1 %copy-start.13 = (s32[2,8,128]{2,1,0:T(8,128)S(1)}, s32[2,8,128]{2,1,0:T(8,128)}, u32[]{:S(2)}) copy-start(s32[2,8,128]{2,1,0:T(8,128)} %get-tuple-element.20.meta) | copy-start | bytes 24580
  47.9 1.0 copy-start.9
  48.8 23.4 %collective-permute-start = (f32[1792,128]{1,0:T(8,128)S(1)}, f32[1792,128]{1,0:T(8,128)S(1)}, u32[]{:S(2)}, u32[]{:S(2)}) collective-permute-start(f32[1792,128]{1,0:T(8,128)S(1)} %get-tuple-element.22), channel_id=1, source_target_pairs={{0,4},{4,0},{1,5},{5,1},{2,6},{6,2},{3,7},{7,3}} | collective-permute-start | bytes 2752520 | tf_op jit(solution)/shard_map/ppermute | solution.py:605
  70.3 0.9 copy-start.10
  71.3 0.9 copy-start.11
  72.2 0.9 copy-start.15
  133.8 1.2 copy-start
  135.0 0.8 copy-start.8
  135.8 0.7 copy-start.14
  147.9 22.9 %copy-start.3 = (f32[2,896,256]{2,1,0:T(8,128)S(1)}, f32[2,896,256]{2,1,0:T(8,128)}, u32[]{:S(2)}) copy-start(f32[2,896,256]{2,1,0:T(8,128)} %refs_7_.3) | copy-start | bytes 5505028
  147.9 22.9 %copy-start.4 = (s32[2,16,512]{1,2,0:T(8,128)S(1)}, s32[2,16,512]{1,2,0:T(8,128)}, u32[]{:S(2)}) copy-start(s32[2,16,512]{1,2,0:T(8,128)} %copy.15) | copy-start | bytes 196612
  147.9 22.9 %copy-start.5 = (s32[2,8,512]{1,2,0:T(8,128)S(1)}, s32[2,8,512]{1,2,0:T(8,128)}, u32[]{:S(2)}) copy-start(s32[2,8,512]{1,2,0:T(8,128)} %copy.14) | copy-start | bytes 98308
  147.9 22.9 %collective-permute-start.1 = (f32[1792,128]{1,0:T(8,128)S(1)}, f32[1792,128]{1,0:T(8,128)S(1)}, u32[]{:S(2)}, u32[]{:S(2)}) collective-permute-start(f32[1792,128]{1,0:T(8,128)S(1)} %get-tuple-element.26), channel_id=1, source_target_pairs={{0,4},{4,0},{1,5},{5,1},{2,6},{6,2},{3,7},{7,3}} | collective-permute-start | bytes 2752520 | tf_op jit(solution)/shard_map/ppermute | solution.py:605

commit v2 on v1

--- a/solution.py
+++ b/solution.py
@@ -23,12 +23,12 @@
 PAIRS = 1024
 FF = 128
 NW = 32
-MC = 32
 CM = 384
 PARTS = 2
 NR = PAIRS // PARTS
 PR = 3 * NR + NR // 2
-PAD = MC
+PAD = 64
+STEP_LOG = (6, 5)
 MIB = 1024 * 1024
 
 
@@ -321,10 +321,15 @@
     )(x, cache_len, id_t, *hbm)
 
 
-def expert_kernel(layer, part, a_ref, meta, pos_ref, w1_ref, w3_ref, w2_ref, mine_ref, theirs_ref,
-                  w1b, w3b, w2b, u, xs, ym, yt, tail, w_sem, o_sem):
+def expert_kernel(layer, part, meta, a_hbm, pos_hbm, w1_ref, w3_ref, w2_ref, mine_ref, theirs_ref,
+                  w1b, w3b, w2b, a_ref, pos_ref, u, xs, ym, yt, tail, w_sem, o_sem, i_sem):
     p = lax.axis_index("pool")
+    stage = [pltpu.make_async_copy(a_hbm, a_ref, i_sem.at[0]), pltpu.make_async_copy(pos_hbm.at[layer], pos_ref, i_sem.at[1])]
+    for cp in stage:
+        cp.start()
     r0 = part * NR
+    log_mc = STEP_LOG[part]
+    MC = 1 << log_mc
     lo, hi = meta[layer, 3 + part, 0], meta[layer, 3 + part, 1]
     odd = (hi - lo) & 1
     lo, hi = jnp.where((odd == 1) & (hi == NE), lo - 1, lo), jnp.where((odd == 1) & (hi < NE), hi + 1, hi)
@@ -341,13 +346,15 @@
 
     lax.fori_loop(lo, jnp.minimum(lo + NW, hi), start, 0)
 
+    for cp in stage:
+        cp.wait()
     u[...] = rms(a_ref[...]).astype(BF16)
 
     def dispatch(i, carry):
         row = iota((256, ALL), 0) + i * 256
         hit = jnp.zeros((256, ALL), F32)
         for k in range(8):
-            hit = jnp.where(pos_ref[layer, k:k + 1, :] == row, 1.0, hit)
+            hit = jnp.where(pos_ref[k:k + 1, :] == row, 1.0, hit)
         xs[pl.ds(pl.multiple_of(i * 256, 256), 256), :] = mm(hit.astype(BF16), u[...]).astype(BF16)
         return carry
 
@@ -356,14 +363,15 @@
     def rows_at(i, j):
         slot = i & (NW - 1)
         rows = xs[pl.ds(pl.multiple_of(meta[layer, 1, i] * 16 + j * MC, 16), MC), :]
-        act = (jax.nn.silu(mm(rows, w1b[slot])) * mm(rows, w3b[slot])).astype(BF16)
+        both = mm(rows, jnp.concatenate([w1b[slot], w3b[slot]], axis=1))
+        act = (jax.nn.silu(both[:, :FF]) * both[:, FF:]).astype(BF16)
         return mm(act, w2b[slot]), pl.ds(jnp.minimum(meta[layer, 2, i] + j * MC - r0, NR) + PAD, MC)
 
     def targets(to):
         return [ym.at[t // 3, t % 3, to] for t in range(6)] + [yt.at[to]]
 
     def first_step(i):
-        return jnp.maximum(r0 - meta[layer, 2, i], 0) >> 5
+        return jnp.maximum(r0 - meta[layer, 2, i], 0) >> log_mc
 
     def more_steps(i):
         n, offc, first = meta[layer, 0, i], meta[layer, 2, i], first_step(i)
@@ -375,7 +383,7 @@
                 ref[...] = jnp.where(keep, y[:, t * 128:(t + 1) * 128], ref[...])
             return carry
 
-        lax.fori_loop(first + 1, (jnp.minimum(n, r0 + NR - offc) + MC - 1) >> 5, step, 0)
+        lax.fori_loop(first + 1, (jnp.minimum(n, r0 + NR - offc) + MC - 1) >> log_mc, step, 0)
 
     def expert_pair(h, carry):
         pair = [lo + 2 * h, lo + 2 * h + 1]
@@ -418,28 +426,30 @@
         functools.partial(expert_kernel, layer, part),
         name=f"experts_{layer}_{part}",
         out_shape=[jax.ShapeDtypeStruct((PR, 128), F32)] * 2,
-        in_specs=[vm, sm, vm, hb, hb, hb],
+        in_specs=[sm, anywhere, anywhere, hb, hb, hb],
         out_specs=[anywhere, anywhere],
         scratch_shapes=[
             pltpu.VMEM((NW, D, FF), BF16), pltpu.VMEM((NW, D, FF), BF16), pltpu.VMEM((NW, FF, D), BF16),
+            pltpu.VMEM((ALL, D), BF16), pltpu.VMEM((16, ALL), I32),
             pltpu.VMEM((ALL, D), BF16), pltpu.VMEM((2304, D), BF16),
             pltpu.VMEM((2, 3, NR + 2 * PAD, 128), F32), pltpu.VMEM((NR + 2 * PAD, 128), F32),
             pltpu.VMEM((2, NR // 2, 128), F32),
-            dma((3, NW)), dma((2, 4)),
+            dma((3, NW)), dma((2, 4)), dma((2,)),
         ],
-        compiler_params=pltpu.CompilerParams(vmem_limit_bytes=38 * MIB),
+        compiler_params=pltpu.CompilerParams(vmem_limit_bytes=61 * MIB),
         cost_estimate=pl.CostEstimate(flops=4_000_000_000, bytes_accessed=44_000_000 // PARTS, transcendentals=PAIRS * FF // PARTS),
-    )(a_all, meta, pos, w1, w3, w2)
+    )(meta, a_all, pos, w1, w3, w2)
 
 
 def merge_steps(layer, devs, ins, x_ref, scr, beside):
-    a_ref, id_ref, pos_ref, mine0_ref, far0_ref, mine1_ref, theirs1_ref, wr_ref = ins
-    (y_own, y_far, wr, gate, base, acc, back, xsend, xfar,
+    a_hbm, id_hbm, pos_hbm, mine0_ref, far0_ref, mine1_ref, theirs1_ref, wr_ref = ins
+    (a_ref, id_ref, pos_ref, y_own, y_far, wr, gate, base, acc, back, xsend, xfar,
      l_sem, ys_sem, yr_sem, bs_sem, br_sem, fs_sem, fr_sem) = scr
     p, e, e_x, e_d, e_z, dev_y, dev_x, dev_d, dev_z, dev_yx = devs
     loads = [pltpu.make_async_copy(src, dst, l_sem.at[i])
              for i, (src, dst) in enumerate(((wr_ref.at[layer], wr), (mine0_ref, y_own.at[0]), (far0_ref, y_far.at[0]),
-                                             (mine1_ref, y_own.at[1])))]
+                                             (mine1_ref, y_own.at[1]), (a_hbm, a_ref), (id_hbm.at[layer], id_ref),
+                                             (pos_hbm.at[layer], pos_ref)))]
     for cp in loads:
         cp.start()
     entry_barrier((dev_y, dev_x, dev_d, dev_z, dev_yx))
@@ -450,7 +460,8 @@
         cp.start()
     beside()
 
-    loads[0].wait()
+    for i in (0, 4, 5, 6):
+        loads[i].wait()
     u = rms(a_ref[...]).astype(BF16)
     logits = jnp.zeros((ALL, 256), F32)
     rest = wr[...]
@@ -459,12 +470,12 @@
         rest = rest - part.astype(F32)
         logits = logits + mm(u, part)
     col = iota((ALL, 256), 1)
-    g = [jnp.sum(jnp.where(id_ref[layer, :, k:k + 1] == col, logits, 0.0), axis=1, keepdims=True) for k in range(8)]
+    g = [jnp.sum(jnp.where(id_ref[:, k:k + 1] == col, logits, 0.0), axis=1, keepdims=True) for k in range(8)]
     top = functools.reduce(jnp.maximum, g)
     g = [jnp.exp(v - top) for v in g]
     total = functools.reduce(jnp.add, g)
     g = [v / total for v in g]
-    pos = [pos_ref[layer, :, 8 + k:9 + k] for k in range(8)]
+    pos = [pos_ref[:, 8 + k:9 + k] for k in range(8)]
     lane = iota((ALL, 128), 1)
     for c in range(PAIRS // 128):
         w = jnp.zeros((ALL, 128), F32)
@@ -532,7 +543,7 @@
         cp.wait_send()
 
 
-MERGE_IN, MERGE_SCR = 8, 16
+MERGE_IN, MERGE_SCR = 8, 19
 
 
 def merge_last_kernel(layer, *refs):
@@ -551,17 +562,18 @@
 def merge_scratch():
     dma = pltpu.SemaphoreType.DMA
     return [
+        pltpu.VMEM((ALL, D), BF16), pltpu.VMEM((ALL, 8), I32), pltpu.VMEM((ALL, 16), I32),
         pltpu.VMEM((2, PR, 128), F32), pltpu.VMEM((2, PR, 128), F32),
         pltpu.VMEM((D, 256), F32), pltpu.VMEM((3, ALL, PAIRS), BF16),
         pltpu.VMEM((4, ALL, 128), F32), pltpu.VMEM((4, ALL, 128), F32), pltpu.VMEM((4, 3, T, 128), F32),
         pltpu.VMEM((4, T, 128), BF16), pltpu.VMEM((4, T, 128), BF16),
-        dma((4,)), dma((4,)), dma((4,)), dma((4, 3)), dma((4, 3)), dma((4,)), dma((4,)),
+        dma((7,)), dma((4,)), dma((4,)), dma((4, 3)), dma((4, 3)), dma((4,)), dma((4,)),
     ]
 
 
 def merge(layer, last, ins, cache_len, hbm):
     vm, sm, hb, anywhere = (pl.BlockSpec(memory_space=m) for m in (pltpu.VMEM, pltpu.SMEM, pltpu.HBM, pl.ANY))
-    in_specs = [vm, vm, vm, anywhere, anywhere, anywhere, anywhere, hb]
+    in_specs = [anywhere] * 7 + [hb]
     params = functools.partial(pltpu.CompilerParams, collective_id=1 + layer, has_side_effects=True)
     if last:
         return pl.pallas_call(
@@ -571,7 +583,7 @@
             in_specs=in_specs,
             out_specs=vm,
             scratch_shapes=merge_scratch(),
-            compiler_params=params(vmem_limit_bytes=24 * MIB),
+            compiler_params=params(vmem_limit_bytes=61 * MIB),
         )(*ins)
     return pl.pallas_call(
         functools.partial(merge_next_kernel, layer),

time: 206 us -> 208 us (level)
  Pallas kernels: 190 us -> 200 us
  local copies, waits for them, and re-layouts: 11.9 us -> 4.59 us
    pallas_call x4, Pallas kernels: 63.5 us -> 74.7 us  [experts(): pl.pallas_call(functools.partial(expert_kernel, layer, part), name=f'expe...]
    unnamed x35 -> x7, local copies, waits for them, and re-layouts: 9.88 us -> 2.58 us
  transfers between devices with their start and end apart: 2 -> 2, of which waited for: 0 -> 0; matrix products, arithmetic and copies ran while one was open for 1% -> 1% of each run, Pallas kernels for 20% -> 25%
where the time goes in v2:
time: 208 us; the launch traced here: 207 us
  Pallas kernels  200 us (96%)
  local copies, waits for them, and re-layouts  4.59 us (2%)
    pallas_call x4, Pallas kernels, experts(): pl.pallas_call(functools.partial(expert_kernel, layer, part), name=f'expe...  74.7 us
    pallas_call x1, Pallas kernels, merge(): pl.pallas_call(functools.partial(merge_next_kernel, layer), name=f'merge_...  59.8 us
    pallas_call x1, Pallas kernels, attention(): pl.pallas_call(attn_kernel, name='attn_0', out_shape=[jax.ShapeDtypeStruc...  33.7 us
    pallas_call x1, Pallas kernels, merge(): pl.pallas_call(functools.partial(merge_last_kernel, layer), name=f'merge_...  32.2 us
  transfers between devices with their start and end apart: 2, of which 0 were waited for; matrix products, arithmetic and copies ran while one was open for 1% of the time, Pallas kernels for 25%

profile of v2, /device:TPU:0, one launch (start us, length us, event | category | flops | bytes accessed | tf_op | source)
XLA Modules:
  0.0 206.9 jit_solution(10726219318797743504)
XLA Ops:
  0.0 33.7 %attn_0.1 = (bf16[512,896]{1,0:T(8,128)(2,1)}, s32[2,8,512]{2,1,0:T(8,128)}, s32[2,8,128]{2,1,0:T(8,128)}, s32[2,16,512]{2,1,0:T(8,128)}) custom-call(bf16[128,896]{1,0:T(8,128)(2,1)} %x_ref.1, s32[128]{0:T(128)} %refs_8_.1, s32[2,8,128]{2,1,0:T(8,128)} %bitcast.13, bf16[2,128,512,128]{3,2,1,0:T(8,128)(2,1)} %bitcast.5, bf16[2,128,512,128]{3,2,1,0:T(8,128)(2,1)} %bitcast.7, ...), custom_call_target="tpu_custom_call" | custom-call | tf_op jit(solution)/shard_map/attn_0/pallas_call | solution.py:312
  33.7 0.0 copy-start
  33.7 0.0 copy-start.2
  33.8 11.4 %experts_0_0.1 = (f32[1792,128]{1,0:T(8,128)}, f32[1792,128]{1,0:T(8,128)}) custom-call(s32[2,8,128]{2,1,0:T(8,128)} %get-tuple-element.20.meta, bf16[512,896]{1,0:T(8,128)(2,1)} %get-tuple-element.17.a_hbm.refs_0_, s32[2,16,512]{2,1,0:T(8,128)} %get-tuple-element.19.pos_hbm, bf16[2,64,896,128]{3,2,1,0:T(8,128)(2,1)} %w1_ref.7, ...), custom_call_target="tpu_custom_call" | custom-call | flops 4000000000 | bytes 22000000 | tf_op jit(solution)/shard_map/experts_0_0/pallas_call | solution.py:425
  45.2 0.7 collective-permute-start
  45.9 0.0 copy-done
  45.9 1.0 copy.15
  46.9 0.0 copy-done.2
  46.9 1.0 copy.14
  47.9 25.6 %experts_0_1.1 = (f32[1792,128]{1,0:T(8,128)}, f32[1792,128]{1,0:T(8,128)}) custom-call(s32[2,8,128]{2,1,0:T(8,128)} %get-tuple-element.20.meta, bf16[512,896]{1,0:T(8,128)(2,1)} %get-tuple-element.17.a_hbm.refs_0_, s32[2,16,512]{2,1,0:T(8,128)} %get-tuple-element.19.pos_hbm, bf16[2,64,896,128]{3,2,1,0:T(8,128)(2,1)} %w1_ref.7, ...), custom_call_target="tpu_custom_call" | custom-call | flops 4000000000 | bytes 22000000 | tf_op jit(solution)/shard_map/experts_0_1/pallas_call | solution.py:425
  73.5 0.0 collective-permute-done.refs_4_
  73.6 59.8 %merge_attn_0.1.a_hbm.refs_0_ = bf16[512,896]{1,0:T(8,128)(2,1)} custom-call(bf16[512,896]{1,0:T(8,128)(2,1)} %get-tuple-element.17.a_hbm.refs_0_, s32[2,512,8]{2,1,0:T(8,128)} %bitcast.11, s32[2,512,16]{2,1,0:T(8,128)} %bitcast.9, f32[1792,128]{1,0:T(8,128)} %get-tuple-element.21.refs_3_, f32[1792,128]{1,0:T(8,128)} %collective-permute-done.refs_4_, ...), custom_call_target="tpu_custom_call" | custom-call | tf_op jit(solution)/shard_map/merge_attn_0/pallas_call | solution.py:588
  133.4 11.4 %experts_1_0.1 = (f32[1792,128]{1,0:T(8,128)}, f32[1792,128]{1,0:T(8,128)}) custom-call(s32[2,8,128]{2,1,0:T(8,128)} %get-tuple-element.20.meta, bf16[512,896]{1,0:T(8,128)(2,1)} %merge_attn_0.1.a_hbm.refs_0_, s32[2,16,512]{2,1,0:T(8,128)} %get-tuple-element.19.pos_hbm, bf16[2,64,896,128]{3,2,1,0:T(8,128)(2,1)} %w1_ref.7, bf16[2,64,896,128]{3,2,1,0:T(8,128)(2,1)} %w3_ref.7, ...), custom_call_target="tpu_custom_call" | custom-call | flops 4000000000 | bytes 22000000 | tf_op jit(solution)/shard_map/experts_1_0/pallas_call | solution.py:425
  144.7 1.0 collective-permute-start.1
  145.7 26.3 %experts_1_1.1 = (f32[1792,128]{1,0:T(8,128)}, f32[1792,128]{1,0:T(8,128)}) custom-call(s32[2,8,128]{2,1,0:T(8,128)} %get-tuple-element.20.meta, bf16[512,896]{1,0:T(8,128)(2,1)} %merge_attn_0.1.a_hbm.refs_0_, s32[2,16,512]{2,1,0:T(8,128)} %get-tuple-element.19.pos_hbm, bf16[2,64,896,128]{3,2,1,0:T(8,128)(2,1)} %w1_ref.7, bf16[2,64,896,128]{3,2,1,0:T(8,128)(2,1)} %w3_ref.7, ...), custom_call_target="tpu_custom_call" | custom-call | flops 4000000000 | bytes 22000000 | tf_op jit(solution)/shard_map/experts_1_1/pallas_call | solution.py:425
  172.1 0.0 collective-permute-done.1.refs_4_
  172.1 0.0 copy-start.1
  172.1 0.9 copy-done.1
  173.0 32.2 %merge_1.1 = bf16[128,896]{1,0:T(8,128)(2,1)} custom-call(bf16[512,896]{1,0:T(8,128)(2,1)} %merge_attn_0.1.a_hbm.refs_0_, s32[2,512,8]{2,1,0:T(8,128)} %bitcast.12, s32[2,512,16]{2,1,0:T(8,128)} %bitcast.10, f32[1792,128]{1,0:T(8,128)} %get-tuple-element.25.refs_3_, f32[1792,128]{1,0:T(8,128)} %copy-done.1, f32[1792,128]{1,0:T(8,128)} %get-tuple-element.27.refs_5_, ...), custom_call_target="tpu_custom_call" | custom-call | tf_op jit(solution)/shard_map/merge_1/pallas_call | solution.py:579
  205.2 1.6 copy.17
Async XLA Ops:
  33.7 12.2 %copy-start = (s32[2,16,512]{2,1,0:T(8,128)S(1)}, s32[2,16,512]{2,1,0:T(8,128)}, u32[]{:S(2)}) copy-start(s32[2,16,512]{2,1,0:T(8,128)} %get-tuple-element.19.pos_hbm) | copy-start | bytes 196612
  33.7 13.2 %copy-start.2 = (s32[2,8,512]{2,1,0:T(8,128)S(1)}, s32[2,8,512]{2,1,0:T(8,128)}, u32[]{:S(2)}) copy-start(s32[2,8,512]{2,1,0:T(8,128)} %get-tuple-element.18) | copy-start | bytes 98308
  45.2 28.4 %collective-permute-start = (f32[1792,128]{1,0:T(8,128)}, f32[1792,128]{1,0:T(8,128)}, u32[]{:S(2)}, u32[]{:S(2)}) collective-permute-start(f32[1792,128]{1,0:T(8,128)} %get-tuple-element.22), channel_id=1, source_target_pairs={{0,4},{4,0},{1,5},{5,1},{2,6},{6,2},{3,7},{7,3}} | collective-permute-start | bytes 2752520 | tf_op jit(solution)/shard_map/ppermute | solution.py:617
  144.7 27.3 %collective-permute-start.1 = (f32[1792,128]{1,0:T(8,128)}, f32[1792,128]{1,0:T(8,128)S(1)}, u32[]{:S(2)}, u32[]{:S(2)}) collective-permute-start(f32[1792,128]{1,0:T(8,128)} %get-tuple-element.26), channel_id=1, source_target_pairs={{0,4},{4,0},{1,5},{5,1},{2,6},{6,2},{3,7},{7,3}} | collective-permute-start | bytes 2752520 | tf_op jit(solution)/shard_map/ppermute | solution.py:617
  172.1 0.9 copy-start.1

commit v3 on v2

--- a/solution.py
+++ b/solution.py
@@ -17,6 +17,8 @@
 ROWS = POS * KV
 CH = 8
 NCH = T // CH
+HC = NCH // 4
+ST = HC * CH
 NB = 8
 ALL = 4 * T
 NE = 64
@@ -162,7 +164,8 @@
             rows = pl.ds(pl.multiple_of(c * (CH * H), CH * H), CH * H)
             return remote(num.at[rows], nrec.at[rows], ns_sem.at[c], nr_sem.at[c], dev_y)
 
-        stat_copy = remote(ssend, srec, ss_sem, sr_sem, dev_y)
+        def stat_copy(h):
+            return remote(ssend.at[h], srec.at[h], ss_sem.at[h], sr_sem.at[h], dev_y)
 
         def chunk(c, carry):
             slot = c & (nb - 1)
@@ -198,72 +201,82 @@
                 for cp in kv_copies(c + nb):
                     cp.start()
 
-            @pl.when(c == NCH // 2 - 1)
-            def _():
-                ssend[0], ssend[1] = m_all, l_all
+            for h in range(2):
+                @pl.when(c == (h + 1) * HC - 1)
+                def _():
+                    ssend[h, 0], ssend[h, 1] = m_all, l_all
 
             @pl.when((c >= 1) & (c <= NCH // 2))
             def _():
                 num_copy(c - 1).start()
 
-            @pl.when(c == NCH // 2)
-            def _():
-                stat_copy.start()
+            for h in range(2):
+                @pl.when(c == (h + 1) * HC)
+                def _():
+                    stat_copy(h).start()
 
             return carry
 
-        stat[...] = jnp.zeros_like(stat)
-        lax.fori_loop(0, NCH, chunk, 0)
-
-        weights[3].wait()
-        stat_copy.wait()
-        m_own, l_own, s_new = stat[0], stat[1], stat[2]
-        m_far = pltpu.roll(srec[0], HALF, axis=1)
-        l_far = pltpu.roll(srec[1], HALF, axis=1)
-        m = jnp.maximum(m_own, m_far)
-        w_own, w_far, w_new = jnp.exp(m_own - m), jnp.exp(m_far - m), jnp.exp(s_new - m)
-        denom = l_own * w_own + l_far * w_far + w_new
-        c_own, c_far, c_new = w_own / denom, w_far / denom, w_new / denom
-
-        def combine(c, carry):
-            num_copy(c).wait()
-            for j in range(CH):
-                i = c * CH + j
-                pick = lane == HALF + i
-                own, far, new = [jnp.sum(jnp.where(pick, v, 0.0), axis=1, keepdims=True) for v in (c_own, c_far, c_new)]
-                there = pl.ds(pl.multiple_of(i * H, H), H)
-                here = pl.ds(pl.multiple_of((HALF + i) * H, H), H)
-                num[here, :] = num[here, :] * own + nrec[there, :] * far + heads_of(vn2d, p * HALF + i) * new
-            return carry
-
-        lax.fori_loop(0, NCH // 2, combine, 0)
-
-        proj = jnp.zeros((HALF, D), F32)
-        for hp in range(H // 2):
-            pair = jnp.concatenate([num[pl.ds(HALF * H + hp * 2 + i, HALF, stride=H), :].astype(BF16) for i in range(2)], axis=1)
-            proj = proj + mm(pair, wo_v[hp * 256:(hp + 1) * 256, :])
-        mine = pl.ds(pl.multiple_of(p * HALF, HALF), HALF)
-
-        def rows(pp, ee):
-            return pl.ds(pl.multiple_of(ee * T + pp * HALF, HALF), HALF)
-
-        a_ref[rows(p, e), :] = (x_ref[mine, :].astype(F32) + proj).astype(BF16)
-
-        def gather(i, pp, ee, dev):
-            block = a_ref.at[rows(pp, ee)]
-            cp = remote(block, block, gs_sem.at[i], gr_sem.at[i], dev)
+        def rows(pp, ee, h):
+            return pl.ds(pl.multiple_of(ee * T + pp * HALF + h * ST, ST), ST)
+
+        def gather(h, i, pp, ee, dev):
+            block = a_ref.at[rows(pp, ee, h)]
+            cp = remote(block, block, gs_sem.at[h, i], gr_sem.at[h, i], dev)
             cp.start()
             return cp
 
-        copies = [gather(0, p, e, dev_yx), gather(1, p, e, dev_x), gather(2, p, e, dev_y), gather(3, p, e, dev_d)]
+        def finish(h):
+            stat_copy(h).wait()
+            m_own, l_own, s_new = stat[0], stat[1], stat[2]
+            m_far = pltpu.roll(srec[h, 0], HALF, axis=1)
+            l_far = pltpu.roll(srec[h, 1], HALF, axis=1)
+            m = jnp.maximum(m_own, m_far)
+            w_own, w_far, w_new = jnp.exp(m_own - m), jnp.exp(m_far - m), jnp.exp(s_new - m)
+            denom = l_own * w_own + l_far * w_far + w_new
+            c_own, c_far, c_new = w_own / denom, w_far / denom, w_new / denom
+
+            def combine(c, carry):
+                num_copy(c).wait()
+                for j in range(CH):
+                    i = c * CH + j
+                    pick = lane == HALF + i
+                    own, far, new = [jnp.sum(jnp.where(pick, v, 0.0), axis=1, keepdims=True) for v in (c_own, c_far, c_new)]
+                    there = pl.ds(pl.multiple_of(i * H, H), H)
+                    here = pl.ds(pl.multiple_of((HALF + i) * H, H), H)
+                    num[here, :] = num[here, :] * own + nrec[there, :] * far + heads_of(vn2d, p * HALF + i) * new
+                return carry
+
+            lax.fori_loop(h * HC, (h + 1) * HC, combine, 0)
+            proj = jnp.zeros((ST, D), F32)
+            first = (HALF + h * ST) * H
+            for hp in range(H // 2):
+                pair = jnp.concatenate([num[pl.ds(first + hp * 2 + i, ST, stride=H), :].astype(BF16) for i in range(2)], axis=1)
+                proj = proj + mm(pair, wo_v[hp * 256:(hp + 1) * 256, :])
+            mine = pl.ds(pl.multiple_of(p * HALF + h * ST, ST), ST)
+            a_ref[rows(p, e, h), :] = (x_ref[mine, :].astype(F32) + proj).astype(BF16)
+            return [gather(h, i, p, e, dev) for i, dev in enumerate((dev_yx, dev_x, dev_y, dev_d))]
+
+        def forward(h, copies):
+            for i, pp, ee in ((2, 1 - p, e), (1, p, e_x), (0, 1 - p, e_x)):
+                copies[i].wait_recv()
+                copies.append(gather(h, len(copies), pp, ee, dev_d))
+
+        stat[...] = jnp.zeros_like(stat)
+        split = NCH - HC
+        lax.fori_loop(0, split, chunk, 0)
+        weights[3].wait()
+        early = finish(0)
+        lax.fori_loop(split, NCH, chunk, 0)
+        late = finish(1)
         between()
-        for i, pp, ee in ((2, 1 - p, e), (1, p, e_x), (0, 1 - p, e_x)):
-            copies[i].wait_recv()
-            copies.append(gather(len(copies), pp, ee, dev_d))
-        for i in range(3, 7):
-            copies[i].wait_recv()
-        for cp in copies:
-            cp.wait_send()
+        forward(0, early)
+        forward(1, late)
+        for copies in (early, late):
+            for cp in copies[3:]:
+                cp.wait_recv()
+            for cp in copies:
+                cp.wait_send()
 
     return start, run
 
@@ -300,8 +313,8 @@
         pltpu.VMEM((H * HD, D), BF16),
         pltpu.VMEM((T * H, HD), F32), pltpu.VMEM((T * KV, HD), F32), pltpu.VMEM((T * KV, HD), F32),
         pltpu.VMEM((T * H, HD), F32), pltpu.VMEM((HALF * H, HD), F32),
-        pltpu.VMEM((3, H, T), F32), pltpu.VMEM((2, H, T), F32), pltpu.VMEM((2, H, T), F32),
-        dma((2, nb)), dma((4,)), dma((NCH // 2,)), dma((NCH // 2,)), dma(()), dma(()), dma((7,)), dma((7,)),
+        pltpu.VMEM((3, H, T), F32), pltpu.VMEM((2, 2, H, T), F32), pltpu.VMEM((2, 2, H, T), F32),
+        dma((2, nb)), dma((4,)), dma((NCH // 2,)), dma((NCH // 2,)), dma((2,)), dma((2,)), dma((2, 7)), dma((2, 7)),
     ]
 
 
@@ -363,8 +376,7 @@
     def rows_at(i, j):
         slot = i & (NW - 1)
         rows = xs[pl.ds(pl.multiple_of(meta[layer, 1, i] * 16 + j * MC, 16), MC), :]
-        both = mm(rows, jnp.concatenate([w1b[slot], w3b[slot]], axis=1))
-        act = (jax.nn.silu(both[:, :FF]) * both[:, FF:]).astype(BF16)
+        act = (jax.nn.silu(mm(rows, w1b[slot])) * mm(rows, w3b[slot])).astype(BF16)
         return mm(act, w2b[slot]), pl.ds(jnp.minimum(meta[layer, 2, i] + j * MC - r0, NR) + PAD, MC)
 
     def targets(to):
@@ -477,14 +489,17 @@
     g = [v / total for v in g]
     pos = [pos_ref[:, 8 + k:9 + k] for k in range(8)]
     lane = iota((ALL, 128), 1)
-    for c in range(PAIRS // 128):
+    def build(c, carry):
         w = jnp.zeros((ALL, 128), F32)
         for k in range(8):
             w = jnp.where(pos[k] == lane + c * 128, g[k], w)
         for i in range(3):
             part = w.astype(BF16)
             w = w - part.astype(F32)
-            gate[i, :, c * 128:(c + 1) * 128] = part
+            gate[i, :, pl.ds(pl.multiple_of(c * 128, 128), 128)] = part
+        return carry
+
+    lax.fori_loop(0, PAIRS // 128, build, 0)
 
     def mix(h, t):
         b, n = spans[t]
@@ -505,9 +520,25 @@
     def block_of(ee):
         return pl.ds(pl.multiple_of(ee * T, T), T)
 
+    left = iota((T // 2, 128), 1) < 64
+    keep0 = jnp.broadcast_to(p == 0, left.shape)
+
+    def swap(v):
+        return pltpu.roll(v, 64, axis=1)
+
+    def pack(v):
+        top, bot = v[:T // 2], v[T // 2:]
+        return jnp.where(left, jnp.where(keep0, top, swap(top)), jnp.where(keep0, swap(bot), bot))
+
+    def span_of(ee, t):
+        n = T if t < 3 else T // 2
+        return pl.ds(pl.multiple_of(ee * n, n), n), pl.ds(0, n)
+
     def give(t):
-        cps = [remote(acc.at[t, block_of(ee)], back.at[t, i], bs_sem.at[t, i], br_sem.at[t, i], dev)
-               for i, (ee, dev) in enumerate(((e_x, dev_x), (e_z, dev_z), (e_d, dev_d)))]
+        cps = []
+        for i, (ee, dev) in enumerate(((e_x, dev_x), (e_z, dev_z), (e_d, dev_d))):
+            src, dst = span_of(ee, t)
+            cps.append(remote(acc.at[t, src], back.at[t, i, dst], bs_sem.at[t, i], br_sem.at[t, i], dev))
         for cp in cps:
             cp.start()
         return cps
@@ -518,16 +549,23 @@
     def finish(t, cps):
         for cp in cps:
             cp.wait_recv()
-        total = acc[t, block_of(e), :] + back[t, 0] + back[t, 1] + back[t, 2]
-        xsend[t] = (a_ref[block_of(e), cols(p, t)].astype(F32) + total).astype(BF16)
-        cp = remote(xsend.at[t], xfar.at[t], fs_sem.at[t], fr_sem.at[t], dev_y)
+        src, dst = span_of(e, t)
+        total = acc[t, src, :] + back[t, 0, dst, :] + back[t, 1, dst, :] + back[t, 2, dst, :]
+        a_own = a_ref[block_of(e), cols(p, t)].astype(F32)
+        xsend[t, dst, :] = ((a_own if t < 3 else pack(a_own)) + total).astype(BF16)
+        cp = remote(xsend.at[t, dst], xfar.at[t, dst], fs_sem.at[t], fr_sem.at[t], dev_y)
         cp.start()
         return cp
 
     given, sent = [], []
     for t in range(4):
         y_copies[t].wait_recv()
-        acc[t] = base[t] + mix(1, t)
+        full = base[t] + mix(1, t)
+        if t < 3:
+            acc[t] = full
+        else:
+            for b in range(ALL // T):
+                acc[t, b * T // 2:(b + 1) * T // 2, :] = pack(full[b * T:(b + 1) * T])
         given.append(give(t))
         if t >= 1:
             sent.append(finish(t - 1, given[t - 1]))
@@ -537,8 +575,10 @@
         sent[t].wait()
         x_ref[:, cols(1 - p, t)] = xfar[t]
     sent[3].wait()
-    keep_own = (iota((T, 128), 1) // 64) == p
-    x_ref[:, 2 * CM:] = jnp.where(keep_own, xsend[3].astype(F32), xfar[3].astype(F32)).astype(BF16)
+    own, far = xsend[3, :T // 2, :].astype(F32), xfar[3, :T // 2, :].astype(F32)
+    q0, q1 = jnp.where(keep0, own, far), jnp.where(keep0, far, own)
+    x_ref[:T // 2, 2 * CM:] = jnp.where(left, q0, swap(q1)).astype(BF16)
+    x_ref[T // 2:, 2 * CM:] = jnp.where(left, swap(q0), q1).astype(BF16)
     for cp in y_copies + [c for cps in given for c in cps]:
         cp.wait_send()
 

time: 208 us -> 196 us (0.942)
  Pallas kernels: 200 us -> 189 us
    pallas_call x4, Pallas kernels: 74.7 us -> 67.3 us  [experts(): pl.pallas_call(functools.partial(expert_kernel, layer, part), name=f'expe...]
    pallas_call x1, Pallas kernels: 59.8 us -> 57.4 us  [merge(): pl.pallas_call(functools.partial(merge_next_kernel, layer), name=f'merge_...]
  transfers between devices with their start and end apart: 2 -> 2, of which waited for: 0 -> 0; matrix products, arithmetic and copies ran while one was open for 1% -> 1% of each run, Pallas kernels for 25% -> 23%
where the time goes in v3:
time: 196 us; the launch traced here: 195 us
  Pallas kernels  189 us (96%)
  local copies, waits for them, and re-layouts  4.59 us (2%)
    pallas_call x4, Pallas kernels, experts(): pl.pallas_call(functools.partial(expert_kernel, layer, part), name=f'expe...  67.3 us
    pallas_call x1, Pallas kernels, merge(): pl.pallas_call(functools.partial(merge_next_kernel, layer), name=f'merge_...  57.4 us
    pallas_call x1, Pallas kernels, attention(): pl.pallas_call(attn_kernel, name='attn_0', out_shape=[jax.ShapeDtypeStruc...  33 us
    pallas_call x1, Pallas kernels, merge(): pl.pallas_call(functools.partial(merge_last_kernel, layer), name=f'merge_...  31.5 us
  transfers between devices with their start and end apart: 2, of which 0 were waited for; matrix products, arithmetic and copies ran while one was open for 1% of the time, Pallas kernels for 23%

profile of v3, /device:TPU:0, one launch (start us, length us, event | category | flops | bytes accessed | tf_op | source)
XLA Modules:
  0.0 195.4 jit_solution(6459837034505413273)
XLA Ops:
  0.0 33.0 %attn_0.1 = (bf16[512,896]{1,0:T(8,128)(2,1)}, s32[2,8,512]{2,1,0:T(8,128)}, s32[2,8,128]{2,1,0:T(8,128)}, s32[2,16,512]{2,1,0:T(8,128)}) custom-call(bf16[128,896]{1,0:T(8,128)(2,1)} %x_ref.1, s32[128]{0:T(128)} %refs_8_.1, s32[2,8,128]{2,1,0:T(8,128)} %bitcast.13, bf16[2,128,512,128]{3,2,1,0:T(8,128)(2,1)} %bitcast.5, bf16[2,128,512,128]{3,2,1,0:T(8,128)(2,1)} %bitcast.7, ...), custom_call_target="tpu_custom_call" | custom-call | tf_op jit(solution)/shard_map/attn_0/pallas_call | solution.py:325
  33.0 0.0 copy-start
  33.0 0.0 copy-start.2
  33.0 10.7 %experts_0_0.1 = (f32[1792,128]{1,0:T(8,128)}, f32[1792,128]{1,0:T(8,128)}) custom-call(s32[2,8,128]{2,1,0:T(8,128)} %get-tuple-element.20.meta, bf16[512,896]{1,0:T(8,128)(2,1)} %get-tuple-element.17.a_hbm.refs_0_, s32[2,16,512]{2,1,0:T(8,128)} %get-tuple-element.19.pos_hbm, bf16[2,64,896,128]{3,2,1,0:T(8,128)(2,1)} %w1_ref.7, ...), custom_call_target="tpu_custom_call" | custom-call | flops 4000000000 | bytes 22000000 | tf_op jit(solution)/shard_map/experts_0_0/pallas_call | solution.py:437
  43.7 0.8 collective-permute-start
  44.5 0.0 copy-done
  44.5 1.0 copy.15
  45.5 0.0 copy-done.2
  45.5 1.0 copy.14
  46.6 23.2 %experts_0_1.1 = (f32[1792,128]{1,0:T(8,128)}, f32[1792,128]{1,0:T(8,128)}) custom-call(s32[2,8,128]{2,1,0:T(8,128)} %get-tuple-element.20.meta, bf16[512,896]{1,0:T(8,128)(2,1)} %get-tuple-element.17.a_hbm.refs_0_, s32[2,16,512]{2,1,0:T(8,128)} %get-tuple-element.19.pos_hbm, bf16[2,64,896,128]{3,2,1,0:T(8,128)(2,1)} %w1_ref.7, ...), custom_call_target="tpu_custom_call" | custom-call | flops 4000000000 | bytes 22000000 | tf_op jit(solution)/shard_map/experts_0_1/pallas_call | solution.py:437
  69.8 0.0 collective-permute-done.refs_4_
  69.8 57.4 %merge_attn_0.1.a_hbm.refs_0_ = bf16[512,896]{1,0:T(8,128)(2,1)} custom-call(bf16[512,896]{1,0:T(8,128)(2,1)} %get-tuple-element.17.a_hbm.refs_0_, s32[2,512,8]{2,1,0:T(8,128)} %bitcast.11, s32[2,512,16]{2,1,0:T(8,128)} %bitcast.9, f32[1792,128]{1,0:T(8,128)} %get-tuple-element.21.refs_3_, f32[1792,128]{1,0:T(8,128)} %collective-permute-done.refs_4_, ...), custom_call_target="tpu_custom_call" | custom-call | tf_op jit(solution)/shard_map/merge_attn_0/pallas_call | solution.py:628
  127.2 10.8 %experts_1_0.1 = (f32[1792,128]{1,0:T(8,128)}, f32[1792,128]{1,0:T(8,128)}) custom-call(s32[2,8,128]{2,1,0:T(8,128)} %get-tuple-element.20.meta, bf16[512,896]{1,0:T(8,128)(2,1)} %merge_attn_0.1.a_hbm.refs_0_, s32[2,16,512]{2,1,0:T(8,128)} %get-tuple-element.19.pos_hbm, bf16[2,64,896,128]{3,2,1,0:T(8,128)(2,1)} %w1_ref.7, bf16[2,64,896,128]{3,2,1,0:T(8,128)(2,1)} %w3_ref.7, ...), custom_call_target="tpu_custom_call" | custom-call | flops 4000000000 | bytes 22000000 | tf_op jit(solution)/shard_map/experts_1_0/pallas_call | solution.py:437
  137.9 0.8 collective-permute-start.1
  138.7 22.6 %experts_1_1.1 = (f32[1792,128]{1,0:T(8,128)}, f32[1792,128]{1,0:T(8,128)}) custom-call(s32[2,8,128]{2,1,0:T(8,128)} %get-tuple-element.20.meta, bf16[512,896]{1,0:T(8,128)(2,1)} %merge_attn_0.1.a_hbm.refs_0_, s32[2,16,512]{2,1,0:T(8,128)} %get-tuple-element.19.pos_hbm, bf16[2,64,896,128]{3,2,1,0:T(8,128)(2,1)} %w1_ref.7, bf16[2,64,896,128]{3,2,1,0:T(8,128)(2,1)} %w3_ref.7, ...), custom_call_target="tpu_custom_call" | custom-call | flops 4000000000 | bytes 22000000 | tf_op jit(solution)/shard_map/experts_1_1/pallas_call | solution.py:437
  161.3 0.0 collective-permute-done.1.refs_4_
  161.3 0.0 copy-start.1
  161.4 0.9 copy-done.1
  162.3 31.5 %merge_1.1 = bf16[128,896]{1,0:T(8,128)(2,1)} custom-call(bf16[512,896]{1,0:T(8,128)(2,1)} %merge_attn_0.1.a_hbm.refs_0_, s32[2,512,8]{2,1,0:T(8,128)} %bitcast.12, s32[2,512,16]{2,1,0:T(8,128)} %bitcast.10, f32[1792,128]{1,0:T(8,128)} %get-tuple-element.25.refs_3_, f32[1792,128]{1,0:T(8,128)} %copy-done.1, f32[1792,128]{1,0:T(8,128)} %get-tuple-element.27.refs_5_, ...), custom_call_target="tpu_custom_call" | custom-call | tf_op jit(solution)/shard_map/merge_1/pallas_call | solution.py:619
  193.7 1.6 copy.17
Async XLA Ops:
  33.0 11.5 %copy-start = (s32[2,16,512]{2,1,0:T(8,128)S(1)}, s32[2,16,512]{2,1,0:T(8,128)}, u32[]{:S(2)}) copy-start(s32[2,16,512]{2,1,0:T(8,128)} %get-tuple-element.19.pos_hbm) | copy-start | bytes 196612
  33.0 12.5 %copy-start.2 = (s32[2,8,512]{2,1,0:T(8,128)S(1)}, s32[2,8,512]{2,1,0:T(8,128)}, u32[]{:S(2)}) copy-start(s32[2,8,512]{2,1,0:T(8,128)} %get-tuple-element.18) | copy-start | bytes 98308
  43.7 26.0 %collective-permute-start = (f32[1792,128]{1,0:T(8,128)}, f32[1792,128]{1,0:T(8,128)}, u32[]{:S(2)}, u32[]{:S(2)}) collective-permute-start(f32[1792,128]{1,0:T(8,128)} %get-tuple-element.22), channel_id=1, source_target_pairs={{0,4},{4,0},{1,5},{5,1},{2,6},{6,2},{3,7},{7,3}} | collective-permute-start | bytes 2752520 | tf_op jit(solution)/shard_map/ppermute | solution.py:657
  137.9 23.4 %collective-permute-start.1 = (f32[1792,128]{1,0:T(8,128)}, f32[1792,128]{1,0:T(8,128)S(1)}, u32[]{:S(2)}, u32[]{:S(2)}) collective-permute-start(f32[1792,128]{1,0:T(8,128)} %get-tuple-element.26), channel_id=1, source_target_pairs={{0,4},{4,0},{1,5},{5,1},{2,6},{6,2},{3,7},{7,3}} | collective-permute-start | bytes 2752520 | tf_op jit(solution)/shard_map/ppermute | solution.py:657
  161.3 0.9 copy-start.1

commit v4 on v3

--- a/solution.py
+++ b/solution.py
@@ -31,6 +31,7 @@
 PR = 3 * NR + NR // 2
 PAD = 64
 STEP_LOG = (6, 5)
+LN = 128
 MIB = 1024 * 1024
 
 
@@ -68,42 +69,49 @@
                                         device_id=dev, device_id_type=MESH)
 
 
-def route(ids, e, meta, pos):
-    sub = iota((128, ALL), 0)
+def route(ids, e, meta, pos, cols):
+    sub = iota((LN, ALL), 0)
     local = [ids[k:k + 1, :] - e * NE for k in range(8)]
     local = [jnp.where((v >= 0) & (v < NE), v, -1) for v in local]
-    mask = jnp.zeros((128, ALL), F32)
+    mask = jnp.zeros((LN, ALL), F32)
     for v in local:
         mask = jnp.where(v == sub, 1.0, mask)
     mask_b = mask.astype(BF16)
     before = (iota((ALL, ALL), 0) < iota((ALL, ALL), 1)).astype(BF16)
     rank = mm(mask_b, before)
-    n_col = jnp.broadcast_to(jnp.sum(mask, axis=1, keepdims=True), (128, 128)).astype(I32)
+    n_col = jnp.broadcast_to(jnp.sum(mask, axis=1, keepdims=True), (LN, LN)).astype(I32)
     n_row = lax.dot_general(jnp.ones((8, ALL), BF16), mask_b, (((1,), (1,)), ((), ())),
                             preferred_element_type=F32).astype(I32)
-    lower = (iota((128, 128), 1) < iota((128, 128), 0)).astype(BF16)
-    upper = (iota((128, 128), 0) < iota((128, 128), 1)).astype(BF16)
+    lower = (iota((LN, LN), 1) < iota((LN, LN), 0)).astype(BF16)
+    upper = (iota((LN, LN), 0) < iota((LN, LN), 1)).astype(BF16)
     as_b = lambda v: v.astype(F32).astype(BF16)
     off_col = mm(lower, as_b((n_col + 15) >> 4)) * 16.0
     offc_col = mm(lower, as_b(n_col >> 4)) * 16.0 + mm(lower, as_b(n_col & 15))
     off_row = mm(as_b((n_row + 15) >> 4), upper).astype(I32)
     offc_row = (mm(as_b(n_row >> 4), upper) * 16.0 + mm(as_b(n_row & 15), upper)).astype(I32)
-    real = iota((8, 128), 1) < NE
+    real = iota((8, LN), 1) < NE
     table = [n_row, off_row, offc_row]
     for r in range(PARTS):
         lo = jnp.sum(jnp.where(real & (offc_row + n_row <= r * NR), 1.0, 0.0), axis=1, keepdims=True)
         hi = jnp.sum(jnp.where(real & (offc_row < (r + 1) * NR), 1.0, 0.0), axis=1, keepdims=True)
-        table.append(jnp.where(iota((8, 128), 1) == 0, lo, hi).astype(I32))
-    row = iota((8, 128), 0)
-    packed = jnp.zeros((8, 128), I32)
+        table.append(jnp.where(iota((8, LN), 1) == 0, lo, hi).astype(I32))
+    row = iota((8, LN), 0)
+    packed = jnp.zeros((8, LN), I32)
     for i, v in enumerate(table):
         packed = jnp.where(row == i, v, packed)
     meta[...] = packed
-    for base, off in ((0, off_col), (8, offc_col)):
+    found = []
+    for off in (off_col, offc_col):
         where_to = off[:, 0:1] + rank + 1.0
-        for k in range(8):
-            found = jnp.sum(jnp.where(local[k] == sub, where_to, 0.0), axis=0, keepdims=True)
-            pos[base + k:base + k + 1, :] = (found - 1.0).astype(I32)
+        found += [jnp.sum(jnp.where(v == sub, where_to, 0.0), axis=0, keepdims=True) - 1.0 for v in local]
+    for k in range(8):
+        pos[k:k + 1, :] = found[k].astype(I32)
+    row = iota((LN, ALL), 0)
+    table = jnp.zeros((LN, ALL), F32)
+    for k in range(8):
+        table = jnp.where(row == k, found[8 + k], table)
+        table = jnp.where(row == 8 + k, ids[k:k + 1, :].astype(F32), table)
+    cols[...] = table.T.astype(I32)
 
 
 def attn_steps(layer, nb, devs, len_ref, hbm, scr):
@@ -282,7 +290,7 @@
 
 
 def attn_kernel(x_ref, len_ref, idt_ref, *refs):
-    hbm, (a_ref, ida_ref, meta_ref, pos_ref), scr = refs[:6], refs[6:10], refs[10:]
+    hbm, (a_ref, meta_ref, pos_ref, cols_ref), (ida_ref, *scr) = refs[:6], refs[6:10], refs[10:]
     is_sem, ir_sem = scr[-2:]
     devs = peers()
     p, e, e_x, e_d, e_z, dev_y, dev_x, dev_d, dev_z, dev_yx = devs
@@ -300,7 +308,7 @@
         for cp in id_copies:
             cp.wait()
         for n in range(ida_ref.shape[0]):
-            route(ida_ref.at[n], e, meta_ref.at[n], pos_ref.at[n])
+            route(ida_ref.at[n], e, meta_ref.at[n], pos_ref.at[n], cols_ref.at[n])
 
     run(x_ref, a_ref, 2, make_tables)
 
@@ -325,11 +333,11 @@
     return pl.pallas_call(
         attn_kernel,
         name="attn_0",
-        out_shape=[jax.ShapeDtypeStruct((ALL, D), BF16), jax.ShapeDtypeStruct((layers, 8, ALL), I32),
-                   jax.ShapeDtypeStruct((layers, 8, 128), I32), jax.ShapeDtypeStruct((layers, 16, ALL), I32)],
+        out_shape=[jax.ShapeDtypeStruct((ALL, D), BF16), jax.ShapeDtypeStruct((layers, 8, LN), I32),
+                   jax.ShapeDtypeStruct((layers, 8, ALL), I32), jax.ShapeDtypeStruct((layers, ALL, LN), I32)],
         in_specs=[vm, sm, vm] + [hb] * 6,
         out_specs=[vm] * 4,
-        scratch_shapes=attn_scratch(NB) + [dma((3,)), dma((3,))],
+        scratch_shapes=[pltpu.VMEM((layers, 8, ALL), I32)] + attn_scratch(NB) + [dma((3,)), dma((3,))],
         compiler_params=pltpu.CompilerParams(collective_id=0, has_side_effects=True, vmem_limit_bytes=61 * MIB),
     )(x, cache_len, id_t, *hbm)
 
@@ -390,9 +398,9 @@
 
         def step(j, carry):
             y, to = rows_at(i, j)
-            keep = iota((MC, 128), 0) < n - j * MC
+            keep = iota((MC, LN), 0) < n - j * MC
             for t, ref in enumerate(targets(to)):
-                ref[...] = jnp.where(keep, y[:, t * 128:(t + 1) * 128], ref[...])
+                ref[...] = jnp.where(keep, y[:, t * LN:(t + 1) * LN], ref[...])
             return carry
 
         lax.fori_loop(first + 1, (jnp.minimum(n, r0 + NR - offc) + MC - 1) >> log_mc, step, 0)
@@ -405,7 +413,7 @@
         done = [rows_at(i, first_step(i)) for i in pair]
         for y, to in done:
             for t, ref in enumerate(targets(to)):
-                ref[...] = y[:, t * 128:(t + 1) * 128]
+                ref[...] = y[:, t * LN:(t + 1) * LN]
         for i in pair:
             more_steps(i)
         for i in pair:
@@ -421,7 +429,7 @@
             copies.append(pltpu.make_async_copy(ym.at[q, t, pl.ds(PAD, NR)], ref.at[pl.ds(t * NR, NR)], o_sem.at[n, t]))
             copies[-1].start()
     top, bot = yt[PAD:PAD + NR // 2, :], yt[PAD + NR // 2:PAD + NR, :]
-    left = iota((NR // 2, 128), 1) < 64
+    left = iota((NR // 2, LN), 1) < 64
     tail[0] = jnp.where(left, top, pltpu.roll(bot, 64, axis=1))
     tail[1] = jnp.where(left, pltpu.roll(top, 64, axis=1), bot)
     for n, (q, ref) in enumerate(((1 - p, theirs_ref), (p, mine_ref))):
@@ -437,31 +445,30 @@
     return pl.pallas_call(
         functools.partial(expert_kernel, layer, part),
         name=f"experts_{layer}_{part}",
-        out_shape=[jax.ShapeDtypeStruct((PR, 128), F32)] * 2,
+        out_shape=[jax.ShapeDtypeStruct((PR, LN), F32)] * 2,
         in_specs=[sm, anywhere, anywhere, hb, hb, hb],
         out_specs=[anywhere, anywhere],
         scratch_shapes=[
             pltpu.VMEM((NW, D, FF), BF16), pltpu.VMEM((NW, D, FF), BF16), pltpu.VMEM((NW, FF, D), BF16),
-            pltpu.VMEM((ALL, D), BF16), pltpu.VMEM((16, ALL), I32),
+            pltpu.VMEM((ALL, D), BF16), pltpu.VMEM((8, ALL), I32),
             pltpu.VMEM((ALL, D), BF16), pltpu.VMEM((2304, D), BF16),
-            pltpu.VMEM((2, 3, NR + 2 * PAD, 128), F32), pltpu.VMEM((NR + 2 * PAD, 128), F32),
-            pltpu.VMEM((2, NR // 2, 128), F32),
+            pltpu.VMEM((2, 3, NR + 2 * PAD, LN), F32), pltpu.VMEM((NR + 2 * PAD, LN), F32),
+            pltpu.VMEM((2, NR // 2, LN), F32),
             dma((3, NW)), dma((2, 4)), dma((2,)),
         ],
-        compiler_params=pltpu.CompilerParams(vmem_limit_bytes=61 * MIB),
+        compiler_params=pltpu.CompilerParams(vmem_limit_bytes=67043328),
         cost_estimate=pl.CostEstimate(flops=4_000_000_000, bytes_accessed=44_000_000 // PARTS, transcendentals=PAIRS * FF // PARTS),
     )(meta, a_all, pos, w1, w3, w2)
 
 
 def merge_steps(layer, devs, ins, x_ref, scr, beside):
-    a_hbm, id_hbm, pos_hbm, mine0_ref, far0_ref, mine1_ref, theirs1_ref, wr_ref = ins
-    (a_ref, id_ref, pos_ref, y_own, y_far, wr, gate, base, acc, back, xsend, xfar,
+    a_hbm, cols_hbm, mine0_ref, far0_ref, mine1_ref, theirs1_ref, wr_ref = ins
+    (a_ref, cols_ref, y_own, y_far, wr, gate, base, acc, back, xsend, xfar,
      l_sem, ys_sem, yr_sem, bs_sem, br_sem, fs_sem, fr_sem) = scr
     p, e, e_x, e_d, e_z, dev_y, dev_x, dev_d, dev_z, dev_yx = devs
     loads = [pltpu.make_async_copy(src, dst, l_sem.at[i])
              for i, (src, dst) in enumerate(((wr_ref.at[layer], wr), (mine0_ref, y_own.at[0]), (far0_ref, y_far.at[0]),
-                                             (mine1_ref, y_own.at[1]), (a_hbm, a_ref), (id_hbm.at[layer], id_ref),
-                                             (pos_hbm.at[layer], pos_ref)))]
+                                             (mine1_ref, y_own.at[1]), (a_hbm, a_ref), (cols_hbm.at[layer], cols_ref)))]
     for cp in loads:
         cp.start()
     entry_barrier((dev_y, dev_x, dev_d, dev_z, dev_yx))
@@ -472,7 +479,7 @@
         cp.start()
     beside()
 
-    for i in (0, 4, 5, 6):
+    for i in (0, 4, 5):
         loads[i].wait()
     u = rms(a_ref[...]).astype(BF16)
     logits = jnp.zeros((ALL, 256), F32)
@@ -482,24 +489,24 @@
         rest = rest - part.astype(F32)
         logits = logits + mm(u, part)
     col = iota((ALL, 256), 1)
-    g = [jnp.sum(jnp.where(id_ref[:, k:k + 1] == col, logits, 0.0), axis=1, keepdims=True) for k in range(8)]
+    g = [jnp.sum(jnp.where(cols_ref[:, 8 + k:9 + k] == col, logits, 0.0), axis=1, keepdims=True) for k in range(8)]
     top = functools.reduce(jnp.maximum, g)
     g = [jnp.exp(v - top) for v in g]
     total = functools.reduce(jnp.add, g)
     g = [v / total for v in g]
-    pos = [pos_ref[:, 8 + k:9 + k] for k in range(8)]
-    lane = iota((ALL, 128), 1)
+    pos = [cols_ref[:, k:k + 1] for k in range(8)]
+    lane = iota((ALL, LN), 1)
     def build(c, carry):
-        w = jnp.zeros((ALL, 128), F32)
+        w = jnp.zeros((ALL, LN), F32)
         for k in range(8):
-            w = jnp.where(pos[k] == lane + c * 128, g[k], w)
+            w = jnp.where(pos[k] == lane + c * LN, g[k], w)
         for i in range(3):
             part = w.astype(BF16)
             w = w - part.astype(F32)
-            gate[i, :, pl.ds(pl.multiple_of(c * 128, 128), 128)] = part
+            gate[i, :, pl.ds(pl.multiple_of(c * LN, LN), LN)] = part
         return carry
 
-    lax.fori_loop(0, PAIRS // 128, build, 0)
+    lax.fori_loop(0, PAIRS // LN, build, 0)
 
     def mix(h, t):
         b, n = spans[t]
@@ -520,7 +527,7 @@
     def block_of(ee):
         return pl.ds(pl.multiple_of(ee * T, T), T)
 
-    left = iota((T // 2, 128), 1) < 64
+    left = iota((T // 2, LN), 1) < 64
     keep0 = jnp.broadcast_to(p == 0, left.shape)
 
     def swap(v):
@@ -544,7 +551,7 @@
         return cps
 
     def cols(q, t):
-        return pl.ds(pl.multiple_of(q * CM + t * 128, 128), 128) if t < 3 else slice(2 * CM, D)
+        return pl.ds(pl.multiple_of(q * CM + t * LN, LN), LN) if t < 3 else slice(2 * CM, D)
 
     def finish(t, cps):
         for cp in cps:
@@ -583,7 +590,7 @@
         cp.wait_send()
 
 
-MERGE_IN, MERGE_SCR = 8, 19
+MERGE_IN, MERGE_SCR = 7, 18
 
 
 def merge_last_kernel(layer, *refs):
@@ -602,18 +609,18 @@
 def merge_scratch():
     dma = pltpu.SemaphoreType.DMA
     return [
-        pltpu.VMEM((ALL, D), BF16), pltpu.VMEM((ALL, 8), I32), pltpu.VMEM((ALL, 16), I32),
-        pltpu.VMEM((2, PR, 128), F32), pltpu.VMEM((2, PR, 128), F32),
+        pltpu.VMEM((ALL, D), BF16), pltpu.VMEM((ALL, LN), I32),
+        pltpu.VMEM((2, PR, LN), F32), pltpu.VMEM((2, PR, LN), F32),
         pltpu.VMEM((D, 256), F32), pltpu.VMEM((3, ALL, PAIRS), BF16),
-        pltpu.VMEM((4, ALL, 128), F32), pltpu.VMEM((4, ALL, 128), F32), pltpu.VMEM((4, 3, T, 128), F32),
-        pltpu.VMEM((4, T, 128), BF16), pltpu.VMEM((4, T, 128), BF16),
-        dma((7,)), dma((4,)), dma((4,)), dma((4, 3)), dma((4, 3)), dma((4,)), dma((4,)),
+        pltpu.VMEM((4, ALL, LN), F32), pltpu.VMEM((4, ALL, LN), F32), pltpu.VMEM((4, 3, T, LN), F32),
+        pltpu.VMEM((4, T, LN), BF16), pltpu.VMEM((4, T, LN), BF16),
+        dma((6,)), dma((4,)), dma((4,)), dma((4, 3)), dma((4, 3)), dma((4,)), dma((4,)),
     ]
 
 
 def merge(layer, last, ins, cache_len, hbm):
     vm, sm, hb, anywhere = (pl.BlockSpec(memory_space=m) for m in (pltpu.VMEM, pltpu.SMEM, pltpu.HBM, pl.ANY))
-    in_specs = [anywhere] * 7 + [hb]
+    in_specs = [anywhere] * 6 + [hb]
     params = functools.partial(pltpu.CompilerParams, collective_id=1 + layer, has_side_effects=True)
     if last:
         return pl.pallas_call(
@@ -623,7 +630,7 @@
             in_specs=in_specs,
             out_specs=vm,
             scratch_shapes=merge_scratch(),
-            compiler_params=params(vmem_limit_bytes=61 * MIB),
+            compiler_params=params(vmem_limit_bytes=63963136),
         )(*ins)
     return pl.pallas_call(
         functools.partial(merge_next_kernel, layer),
@@ -650,13 +657,12 @@
         v = v_cache.reshape(layers, T, ROWS, HD)
         id_t = jnp.swapaxes(expert_ids, 1, 2)
         hbm = (k, v, w_q, w_k, w_v, w_o)
-        a_all, ids_t, meta, pos_t = attention(hidden, cache_len, id_t, hbm)
-        ids, pos = jnp.swapaxes(ids_t, 1, 2), jnp.swapaxes(pos_t, 1, 2)
+        a_all, meta, pos, cols = attention(hidden, cache_len, id_t, hbm)
         for layer in range(layers):
-            mine0, theirs0 = experts(layer, 0, a_all, meta, pos_t, w_one, w_three, w_two)
+            mine0, theirs0 = experts(layer, 0, a_all, meta, pos, w_one, w_three, w_two)
             far0 = lax.ppermute(theirs0, 'pool', [(0, 1), (1, 0)])
-            mine1, theirs1 = experts(layer, 1, a_all, meta, pos_t, w_one, w_three, w_two)
-            ins = (a_all, ids, pos, mine0, far0, mine1, theirs1, w_router)
+            mine1, theirs1 = experts(layer, 1, a_all, meta, pos, w_one, w_three, w_two)
+            ins = (a_all, cols, mine0, far0, mine1, theirs1, w_router)
             last = layer == layers - 1
             a_all = merge(layer, last, ins, cache_len, hbm)
         return a_all

time: 196 us -> 193 us (0.985)
  Pallas kernels: 189 us -> 186 us
  local copies, waits for them, and re-layouts: 4.59 us -> 1.65 us
    pallas_call x4, Pallas kernels: 67.3 us -> 64.9 us  [experts(): pl.pallas_call(functools.partial(expert_kernel, layer, part), name=f'expe...]
    pallas_call x2 -> x0, local copies, waits for them, and re-layouts: 2.01 us -> none  [attention(): pl.pallas_call(attn_kernel, name='attn_0', out_shape=[jax.ShapeDtypeStruc...]
  transfers between devices with their start and end apart: 2 -> 2, of which waited for: 0 -> 1; matrix products, arithmetic and copies ran while one was open for 1% -> 0% of each run, Pallas kernels for 23% -> 23%
where the time goes in v4:
time: 193 us; the launch traced here: 191 us
  Pallas kernels  186 us (96%)
    pallas_call x4, Pallas kernels, experts(): pl.pallas_call(functools.partial(expert_kernel, layer, part), name=f'expe...  64.9 us
    pallas_call x1, Pallas kernels, merge(): pl.pallas_call(functools.partial(merge_next_kernel, layer), name=f'merge_...  57.4 us
    pallas_call x1, Pallas kernels, attention(): pl.pallas_call(attn_kernel, name='attn_0', out_shape=[jax.ShapeDtypeStruc...  33.1 us
    pallas_call x1, Pallas kernels, merge(): pl.pallas_call(functools.partial(merge_last_kernel, layer), name=f'merge_...  31 us
  transfers between devices with their start and end apart: 2, of which 1 were waited for; matrix products, arithmetic and copies ran while one was open for 0% of the time, Pallas kernels for 23%

profile of v4, /device:TPU:0, one launch (start us, length us, event | category | flops | bytes accessed | tf_op | source)
XLA Modules:
  0.0 190.8 jit_solution(3064674472560946425)
XLA Ops:
  0.0 33.1 %attn_0.1 = (bf16[512,896]{1,0:T(8,128)(2,1)}, s32[2,8,128]{2,1,0:T(8,128)}, s32[2,8,512]{2,1,0:T(8,128)}, s32[2,512,128]{2,1,0:T(8,128)}) custom-call(bf16[128,896]{1,0:T(8,128)(2,1)} %x_ref.1, s32[128]{0:T(128)} %refs_7_.1, s32[2,8,128]{2,1,0:T(8,128)} %bitcast.7, bf16[2,128,512,128]{3,2,1,0:T(8,128)(2,1)} %bitcast.3, bf16[2,128,512,128]{3,2,1,0:T(8,128)(2,1)} %bitcast.5, ...), custom_call_target="tpu_custom_call" | custom-call | tf_op jit(solution)/shard_map/attn_0/pallas_call | solution.py:333
  33.1 11.2 %experts_0_0.1 = (f32[1792,128]{1,0:T(8,128)}, f32[1792,128]{1,0:T(8,128)}) custom-call(s32[2,8,128]{2,1,0:T(8,128)} %get-tuple-element.19.meta, bf16[512,896]{1,0:T(8,128)(2,1)} %get-tuple-element.17.a_hbm.refs_0_, s32[2,8,512]{2,1,0:T(8,128)} %get-tuple-element.20.pos_hbm, bf16[2,64,896,128]{3,2,1,0:T(8,128)(2,1)} %w1_ref.7, ...), custom_call_target="tpu_custom_call" | custom-call | flops 4000000000 | bytes 22000000 | tf_op jit(solution)/shard_map/experts_0_0/pallas_call | solution.py:445
  44.3 0.8 collective-permute-start
  45.1 22.2 %experts_0_1.1 = (f32[1792,128]{1,0:T(8,128)}, f32[1792,128]{1,0:T(8,128)}) custom-call(s32[2,8,128]{2,1,0:T(8,128)} %get-tuple-element.19.meta, bf16[512,896]{1,0:T(8,128)(2,1)} %get-tuple-element.17.a_hbm.refs_0_, s32[2,8,512]{2,1,0:T(8,128)} %get-tuple-element.20.pos_hbm, bf16[2,64,896,128]{3,2,1,0:T(8,128)(2,1)} %w1_ref.7, ...), custom_call_target="tpu_custom_call" | custom-call | flops 4000000000 | bytes 22000000 | tf_op jit(solution)/shard_map/experts_0_1/pallas_call | solution.py:445
  67.3 0.0 collective-permute-done.refs_3_
  67.3 57.4 %merge_attn_0.1.a_hbm.refs_0_ = bf16[512,896]{1,0:T(8,128)(2,1)} custom-call(bf16[512,896]{1,0:T(8,128)(2,1)} %get-tuple-element.17.a_hbm.refs_0_, s32[2,512,128]{2,1,0:T(8,128)} %get-tuple-element.18.refs_1_, f32[1792,128]{1,0:T(8,128)} %get-tuple-element.21.refs_2_, f32[1792,128]{1,0:T(8,128)} %collective-permute-done.refs_3_, ...), custom_call_target="tpu_custom_call" | custom-call | tf_op jit(solution)/shard_map/merge_attn_0/pallas_call | solution.py:635
  124.7 10.7 %experts_1_0.1 = (f32[1792,128]{1,0:T(8,128)}, f32[1792,128]{1,0:T(8,128)}) custom-call(s32[2,8,128]{2,1,0:T(8,128)} %get-tuple-element.19.meta, bf16[512,896]{1,0:T(8,128)(2,1)} %merge_attn_0.1.a_hbm.refs_0_, s32[2,8,512]{2,1,0:T(8,128)} %get-tuple-element.20.pos_hbm, bf16[2,64,896,128]{3,2,1,0:T(8,128)(2,1)} %w1_ref.7, bf16[2,64,896,128]{3,2,1,0:T(8,128)(2,1)} %w3_ref.7, ...), custom_call_target="tpu_custom_call" | custom-call | flops 4000000000 | bytes 22000000 | tf_op jit(solution)/shard_map/experts_1_0/pallas_call | solution.py:445
  135.4 0.8 collective-permute-start.1
  136.2 20.8 %experts_1_1.1 = (f32[1792,128]{1,0:T(8,128)}, f32[1792,128]{1,0:T(8,128)}) custom-call(s32[2,8,128]{2,1,0:T(8,128)} %get-tuple-element.19.meta, bf16[512,896]{1,0:T(8,128)(2,1)} %merge_attn_0.1.a_hbm.refs_0_, s32[2,8,512]{2,1,0:T(8,128)} %get-tuple-element.20.pos_hbm, bf16[2,64,896,128]{3,2,1,0:T(8,128)(2,1)} %w1_ref.7, bf16[2,64,896,128]{3,2,1,0:T(8,128)(2,1)} %w3_ref.7, ...), custom_call_target="tpu_custom_call" | custom-call | flops 4000000000 | bytes 22000000 | tf_op jit(solution)/shard_map/experts_1_1/pallas_call | solution.py:445
  157.0 1.0 collective-permute-done.1.refs_3_
  158.1 31.0 %merge_1.1 = bf16[128,896]{1,0:T(8,128)(2,1)} custom-call(bf16[512,896]{1,0:T(8,128)(2,1)} %merge_attn_0.1.a_hbm.refs_0_, s32[2,512,128]{2,1,0:T(8,128)} %get-tuple-element.18.refs_1_, f32[1792,128]{1,0:T(8,128)} %get-tuple-element.25.refs_2_, f32[1792,128]{1,0:T(8,128)} %collective-permute-done.1.refs_3_, f32[1792,128]{1,0:T(8,128)} %get-tuple-element.27.refs_4_, ...), custom_call_target="tpu_custom_call" | custom-call | tf_op jit(solution)/shard_map/merge_1/pallas_call | solution.py:626
  189.1 1.6 copy.15
Async XLA Ops:
  44.3 23.0 %collective-permute-start = (f32[1792,128]{1,0:T(8,128)}, f32[1792,128]{1,0:T(8,128)}, u32[]{:S(2)}, u32[]{:S(2)}) collective-permute-start(f32[1792,128]{1,0:T(8,128)} %get-tuple-element.22), channel_id=1, source_target_pairs={{0,4},{4,0},{1,5},{5,1},{2,6},{6,2},{3,7},{7,3}} | collective-permute-start | bytes 2752520 | tf_op jit(solution)/shard_map/ppermute | solution.py:663
  135.4 22.7 %collective-permute-start.1 = (f32[1792,128]{1,0:T(8,128)}, f32[1792,128]{1,0:T(8,128)}, u32[]{:S(2)}, u32[]{:S(2)}) collective-permute-start(f32[1792,128]{1,0:T(8,128)} %get-tuple-element.26), channel_id=1, source_target_pairs={{0,4},{4,0},{1,5},{5,1},{2,6},{6,2},{3,7},{7,3}} | collective-permute-start | bytes 2752520 | tf_op jit(solution)/shard_map/ppermute | solution.py:663
